TPU v7x, 32 devices: a whole 2x2x4 slice. The times are simulated.
32 devices in a mesh: dp: 4 (over x, y), tp: 8 (over z, core).
Axes of the slice: x: 2, y: 2, z: 4, core: 2. Of those that a mesh axis runs over, the one named last changes fastest.
Arguments:
- x: bfloat16 [5120, 7168], P(('dp', 'tp')), parts along dimension 0
- dy: bfloat16 [5120, 7168], P(('dp', 'tp')), parts along dimension 0
- pre: bfloat16 [5120, 28672], P('dp', 'tp'), parts along dimension 0
- w_in: bfloat16 [7168, 28672], P(None, 'tp')
- w_down: bfloat16 [28672, 7168], P('tp')
Outputs:
- output 1: bfloat16 [5120, 7168], P(('dp', 'tp')), parts along dimension 0
- output 2: bfloat16 [28672, 28672], P('dp', 'tp'), parts along dimension 0
- output 3: bfloat16 [114688, 7168], P(('dp', 'tp')), parts along dimension 0
There are 4 independent parts. A program takes and returns all parts, laid end to end along the dimension named above; an argument that names none is the same for every part.
All inputs are finite; a program needn't handle non-finite values.
Results may differ from a plain program's by a relative error of at most 0.012.
Values are sent between devices in bfloat16 or wider.
A program may use at most 2 GiB of HBM per device.

v0:
```python
import jax
import jax.numpy as jnp


def act(pre):
    return jax.nn.gelu(pre)


def solution(mesh):
    def step(x, dy, pre, w_in, w_down):
        hidden, back = jax.vjp(act, pre.astype(jnp.float32))
        d_hidden = jnp.dot(dy, w_down.T, preferred_element_type=jnp.float32)
        d_pre = back(d_hidden)[0].astype(jnp.bfloat16)
        dx = jnp.dot(d_pre, w_in.T)
        groups = mesh.shape["dp"]

        def by_group(a, b):
            a, b = (t.reshape(groups, -1, t.shape[-1]) for t in (a, b))
            product = jnp.einsum("gta,gtb->gab", a, b, preferred_element_type=jnp.float32)
            return product.astype(jnp.bfloat16).reshape(-1, b.shape[-1])

        return dx, by_group(x, d_pre), by_group(hidden.astype(jnp.bfloat16), dy)

    return step
```

profile of v0, /device:TPU:0, one launch (start us, length us, event | category | flops | bytes accessed | tf_op | source)
XLA Modules:
  0.0 1214.2 jit_solution(10118412131315653631)
XLA Ops:
  7.2 3.2 copy.27
  10.4 3.2 copy.28
  14.3 2.7 collective-permute-start.8
  16.9 201.3 %all-gather.5.cloned.1.call-done = bf16[1280,7168]{1,0:T(8,128)(2,1)} async-done(((bf16[160,7168]{1,0:T(8,128)(2,1)}), bf16[1280,7168]{1,0:T(8,128)(2,1)}) %all-gather.5.cloned.1.call-update) | async-done | bytes 18350096 | tf_op args[1]
  218.2 90.6 %fusion.40 = (bf16[1,1280,3584]{2,1,0:T(8,128)(2,1)}, bf16[1280,3584]{1,0:T(8,128)(2,1)}) fusion(bf16[1280,3584]{1,0:T(8,128)(2,1)} %param.6, bf16[1280,7168]{1,0:T(8,128)(2,1)} %all-gather.5.cloned.1.call-done, bf16[3584,7168]{1,0:T(8,128)(2,1)} %param.5), kind=kOutput, calls=%fused_computation.59 | convolution fusion | flops 65872199680 | bytes 97255424 | tf_op jit(solution)/dot_general | solution.py:12
  308.8 75.5 %fusion.41 = bf16[1280,7168]{1,0:T(8,128)(2,1)} fusion(bf16[1280,3584]{1,0:T(8,128)(2,1)} %get-tuple-element.71, bf16[7168,3584]{1,0:T(8,128)(2,1)} %param.7), kind=kOutput, calls=%fused_computation.60 | convolution fusion | flops 65766686720 | bytes 78905344 | tf_op jit(solution)/dot_general | solution.py:14
  384.2 285.0 %while.4 = (bf16[1,1280,3584]{2,1,0:T(8,128)(2,1)}, bf16[1,1,160,7168]{3,2,1,0:T(8,128)(2,1)}, f32[1,3584,7168]{2,1,0:T(8,128)}, bf16[1,1,160,7168]{3,2,1,0:T(8,...) while((bf16[1,1280,3584]{2,1,0:T(8,128)(2,1)}, ...), condition=%wide.windowed_dot_general_cond_ag.clone, body=%wide.windowed_dot_general_body_ag.clone.sunk | while | flops 32974176256 | bytes 475267648 | solution.py:19
  387.5 41.5 %fusion.57 = f32[3584,7168,1]{1,0,2:T(8,128)} fusion(bf16[1,1,160,7168]{3,2,1,0:T(8,128)(2,1)} %get-tuple-element.148, bf16[1,1,160,7168]{3,2,1,0:T(8,128)(2,1)} %get-tuple-element.146, s32[]{:T(128)S(6)} %multiply.30, bf16[1,1,1280,3584]{3,2,1,0:T(8,128)(2,1)} %bitcast.106, s32[]{:T(128)S(6)} %multiply.31), kind=kOutput, calls=%fused_computation.7.clone.1 | convolution fusion | flops 16448552960 | bytes 116523016 | tf_op jit(solution)/gta,gtb->gab/dot_general | solution.py:19
  429.0 4.7 collective-permute-done
  433.7 3.7 collective-permute-start.1
  437.5 74.2 %bitcast_add_fusion.6 = f32[1,3584,7168]{2,1,0:T(8,128)} fusion(f32[3584,7168,1]{1,0,2:T(8,128)} %fusion.57, f32[1,3584,7168]{2,1,0:T(8,128)} %get-tuple-element.147, pred[]{:T(512)S(6)} %compare.12, bf16[1,1,160,7168]{3,2,1,0:T(8,128)(2,1)} %collective-permute-done.2, bf16[1,1,160,7168]{3,2,1,0:T(8,128)(2,1)S(1)} %collective-permute-done, ...), kind=kOutput, calls=%fused_computation.clone.3 | convolution fusion | flops 16525623296 | bytes 322043904 | tf_op jit(solution)/gta,gtb->gab/dot_general | solution.py:19
  511.7 3.6 collective-permute-start
  517.8 41.5 %fusion.57 = f32[3584,7168,1]{1,0,2:T(8,128)} fusion(bf16[1,1,160,7168]{3,2,1,0:T(8,128)(2,1)} %get-tuple-element.148, bf16[1,1,160,7168]{3,2,1,0:T(8,128)(2,1)} %get-tuple-element.146, s32[]{:T(128)S(6)} %multiply.30, bf16[1,1,1280,3584]{3,2,1,0:T(8,128)(2,1)} %bitcast.106, s32[]{:T(128)S(6)} %multiply.31), kind=kOutput, calls=%fused_computation.7.clone.1 | convolution fusion | flops 16448552960 | bytes 116523016 | tf_op jit(solution)/gta,gtb->gab/dot_general | solution.py:19
  559.3 5.3 collective-permute-done
  564.7 3.7 collective-permute-start.1
  568.4 100.9 %bitcast_add_fusion.6 = f32[1,3584,7168]{2,1,0:T(8,128)} fusion(f32[3584,7168,1]{1,0,2:T(8,128)} %fusion.57, f32[1,3584,7168]{2,1,0:T(8,128)} %get-tuple-element.147, pred[]{:T(512)S(6)} %compare.12, bf16[1,1,160,7168]{3,2,1,0:T(8,128)(2,1)} %collective-permute-done.2, bf16[1,1,160,7168]{3,2,1,0:T(8,128)(2,1)S(1)} %collective-permute-done, ...), kind=kOutput, calls=%fused_computation.clone.3 | convolution fusion | flops 16525623296 | bytes 322043904 | tf_op jit(solution)/gta,gtb->gab/dot_general | solution.py:19
  669.3 78.7 %copy = bf16[1,3584,7168]{1,2,0:T(8,128)(2,1)} copy(f32[1,3584,7168]{2,1,0:T(8,128)} %get-tuple-element.12) | data formatting | bytes 154140672 | tf_op jit(solution)/gta,gtb->gab/dot_general | solution.py:19
  748.0 409.0 %while.5 = (bf16[1,1280,3584]{2,1,0:T(8,128)(2,1)}, bf16[1,1,160,7168]{3,2,1,0:T(8,128)(2,1)}, f32[1,3584,7168]{2,1,0:T(8,128)}, bf16[1,1,160,7168]{3,2,1,0:T(8,...) while((bf16[1,1280,3584]{2,1,0:T(8,128)(2,1)}, ...), condition=%wide.windowed_dot_general_cond_ag.1.clone, body=%wide.windowed_dot_general_body_ag.1.clone.sunk | while | flops 32974176256 | bytes 484442688 | solution.py:19
  748.3 3.6 collective-permute-start.4
  754.1 41.5 %fusion.60 = f32[3584,7168,1]{1,0,2:T(8,128)} fusion(bf16[1,1,160,7168]{3,2,1,0:T(8,128)(2,1)} %get-tuple-element.181, bf16[1,1,160,7168]{3,2,1,0:T(8,128)(2,1)} %get-tuple-element.179, s32[]{:T(128)S(6)} %multiply.34, bf16[1,1,1280,3584]{3,2,1,0:T(8,128)(2,1)} %bitcast.103, s32[]{:T(128)S(6)} %multiply.35), kind=kOutput, calls=%fused_computation.28.clone.1 | convolution fusion | flops 16448552960 | bytes 116523016 | tf_op jit(solution)/gta,gtb->gab/dot_general | solution.py:19
  795.6 49.5 %collective-permute-done.4 = bf16[1,1,160,7168]{3,2,1,0:T(8,128)(2,1)S(1)} collective-permute-done((bf16[1,1,160,7168]{3,2,1,0:T(8,128)(2,1)}, bf16[1,1,160,7168]{3,2,1,0:T(8,128)(2,1)S(1)}, u32[]{:S(2)}, u32[]{:S(2)}) %collective-permute-start.4) | collective-permute-done | bytes 2293792 | tf_op jit(solution)/gta,gtb->gab/dot_general | solution.py:19
  845.1 3.7 collective-permute-start.5
  848.8 1.9 collective-permute-done.6
  850.7 73.8 %bitcast_add_fusion.7 = f32[1,3584,7168]{2,1,0:T(8,128)} fusion(f32[3584,7168,1]{1,0,2:T(8,128)} %fusion.60, f32[1,3584,7168]{2,1,0:T(8,128)} %get-tuple-element.180, pred[]{:T(512)S(6)} %compare.13, bf16[1,1,160,7168]{3,2,1,0:T(8,128)(2,1)} %collective-permute-done.6, bf16[1,1,160,7168]{3,2,1,0:T(8,128)(2,1)S(1)} %collective-permute-done.4, ...), kind=kOutput, calls=%fused_computation.21.clone.1 | convolution fusion | flops 16525623296 | bytes 322043904 | tf_op jit(solution)/gta,gtb->gab/dot_general | solution.py:19
  924.5 22.4 %collective-permute-done.5 = bf16[1,1,160,7168]{3,2,1,0:T(8,128)(2,1)S(1)} collective-permute-done((bf16[1,1,160,7168]{3,2,1,0:T(8,128)(2,1)S(1)}, bf16[1,1,160,7168]{3,2,1,0:T(8,128)(2,1)S(1)}, u32[]{:S(2)}, u32[]{:S(2)}) %collective-permute-start.5) | collective-permute-done | bytes 2293792 | tf_op jit(solution)/gta,gtb->gab/dot_general | solution.py:19
  946.9 4.2 collective-permute-done.7
  954.2 41.5 %fusion.60 = f32[3584,7168,1]{1,0,2:T(8,128)} fusion(bf16[1,1,160,7168]{3,2,1,0:T(8,128)(2,1)} %get-tuple-element.181, bf16[1,1,160,7168]{3,2,1,0:T(8,128)(2,1)} %get-tuple-element.179, s32[]{:T(128)S(6)} %multiply.34, bf16[1,1,1280,3584]{3,2,1,0:T(8,128)(2,1)} %bitcast.103, s32[]{:T(128)S(6)} %multiply.35), kind=kOutput, calls=%fused_computation.28.clone.1 | convolution fusion | flops 16448552960 | bytes 116523016 | tf_op jit(solution)/gta,gtb->gab/dot_general | solution.py:19
  995.8 55.2 %collective-permute-done.4 = bf16[1,1,160,7168]{3,2,1,0:T(8,128)(2,1)S(1)} collective-permute-done((bf16[1,1,160,7168]{3,2,1,0:T(8,128)(2,1)}, bf16[1,1,160,7168]{3,2,1,0:T(8,128)(2,1)S(1)}, u32[]{:S(2)}, u32[]{:S(2)}) %collective-permute-start.4) | collective-permute-done | bytes 2293792 | tf_op jit(solution)/gta,gtb->gab/dot_general | solution.py:19
  1051.0 3.7 collective-permute-start.5
  1054.7 100.9 %bitcast_add_fusion.7 = f32[1,3584,7168]{2,1,0:T(8,128)} fusion(f32[3584,7168,1]{1,0,2:T(8,128)} %fusion.60, f32[1,3584,7168]{2,1,0:T(8,128)} %get-tuple-element.180, pred[]{:T(512)S(6)} %compare.13, bf16[1,1,160,7168]{3,2,1,0:T(8,128)(2,1)} %collective-permute-done.6, bf16[1,1,160,7168]{3,2,1,0:T(8,128)(2,1)S(1)} %collective-permute-done.4, ...), kind=kOutput, calls=%fused_computation.21.clone.1 | convolution fusion | flops 16525623296 | bytes 322043904 | tf_op jit(solution)/gta,gtb->gab/dot_general | solution.py:19
  1155.7 1.4 copy-done
  1157.1 49.9 %convert_bitcast_fusion = bf16[3584,7168]{1,0:T(8,128)(2,1)} fusion(f32[1,3584,7168]{2,1,0:T(8,128)} %get-tuple-element.13), kind=kLoop, calls=%fused_computation.42 | loop fusion | flops 25690112 | bytes 154140672 | tf_op jit(solution)/reshape | solution.py:20
  (38 shorter events, 4.6 us)
Async XLA Ops:
  7.2 211.1 %all-gather.5.cloned.1.call-start = ((), (), s32[]{:S(2)}) async-start(), calls=%async_computation.1 | async-start | bytes 20643840 | tf_op args[1]
  13.6 1193.3 %reduce-scatter.4.cloned.1.call-start = ((), (), s32[]{:S(2)}) async-start(), calls=%async_computation.2 | async-start | bytes 20643840
  13.7 734.3 %collective-permute-start.9 = (bf16[1,1,160,7168]{3,2,1,0:T(8,128)(2,1)}, bf16[1,1,160,7168]{3,2,1,0:T(8,128)(2,1)}, u32[]{:S(2)}, u32[]{:S(2)}) collective-permute-start(bf16[1,1,160,7168]{3,2,1,0:T(8,128)(2,1)} %bitcast.109), channel_id=11, source_target_pairs={{0,1},{1,2},{2,3},{3,4},{4,5},{5,6},{6,7},{7,0},{8,9},{9,10},{10,1... | collective-permute-start | bytes 6881288 | tf_op jit(solution)/gta,gtb->gab/dot_general | solution.py:19
  14.3 370.0 %collective-permute-start.8 = (bf16[1,1,160,7168]{3,2,1,0:T(8,128)(2,1)}, bf16[1,1,160,7168]{3,2,1,0:T(8,128)(2,1)}, u32[]{:S(2)}, u32[]{:S(2)}) collective-permute-start(bf16[1,1,160,7168]{3,2,1,0:T(8,128)(2,1)} %bitcast.2), channel_id=5, source_target_pairs={{0,1},{1,2},{2,3},{3,4},{4,5},{5,6},{6,7},{7,0},{8,9},{9,10},{10,1... | collective-permute-start | bytes 6881288 | tf_op jit(solution)/gta,gtb->gab/dot_general | solution.py:19
  308.8 75.5 %copy-start.1 = (u32[32]{0:T(128)S(1)}, u32[32]{0:T(128)}, u32[]{:S(2)}) copy-start(u32[32]{0:T(128)} %constant.255) | copy-start | bytes 388
  384.5 49.3 %collective-permute-start = (bf16[1,1,160,7168]{3,2,1,0:T(8,128)(2,1)}, bf16[1,1,160,7168]{3,2,1,0:T(8,128)(2,1)S(1)}, u32[]{:S(2)}, u32[]{:S(2)}) collective-permute-start(bf16[1,1,160,7168]{3,2,1,0:T(8,128)(2,1)} %get-tuple-element.146), channel_id=6, source_target_pairs={{0,7},{1,0},{2,1},{3,2},{4,3},{5,4},{6,5},{7,6},{8,15},{9,8},{10,9... | collective-permute-start | bytes 6881288 | tf_op jit(solution)/gta,gtb->gab/dot_general | solution.py:19
  384.7 52.8 %collective-permute-start.2 = (bf16[1,1,160,7168]{3,2,1,0:T(8,128)(2,1)}, bf16[1,1,160,7168]{3,2,1,0:T(8,128)(2,1)}, u32[]{:S(2)}, u32[]{:S(2)}) collective-permute-start(bf16[1,1,160,7168]{3,2,1,0:T(8,128)(2,1)} %get-tuple-element.148), channel_id=7, source_target_pairs={{0,1},{1,2},{2,3},{3,4},{4,5},{5,6},{6,7},{7,0},{8,9},{9,10},{10,1... | collective-permute-start | bytes 6881288 | tf_op jit(solution)/gta,gtb->gab/dot_general | solution.py:19
  433.7 78.0 %collective-permute-start.1 = (bf16[1,1,160,7168]{3,2,1,0:T(8,128)(2,1)S(1)}, bf16[1,1,160,7168]{3,2,1,0:T(8,128)(2,1)}, u32[]{:S(2)}, u32[]{:S(2)}) collective-permute-start(bf16[1,1,160,7168]{3,2,1,0:T(8,128)(2,1)S(1)} %collective-permute-done), channel_id=8, source_target_pairs={{0,7},{1,0},{2,1},{3,2},{4,3},{5,4},{6,5},{7,6},{8,15},{9,8},{10,9... | collective-permute-start | bytes 6881288 | tf_op jit(solution)/gta,gtb->gab/dot_general | solution.py:19
  437.5 74.2 %collective-permute-start.3 = (bf16[1,1,160,7168]{3,2,1,0:T(8,128)(2,1)}, bf16[1,1,160,7168]{3,2,1,0:T(8,128)(2,1)}, u32[]{:S(2)}, u32[]{:S(2)}) collective-permute-start(bf16[1,1,160,7168]{3,2,1,0:T(8,128)(2,1)} %collective-permute-done.2), channel_id=9, source_target_pairs={{0,1},{1,2},{2,3},{3,4},{4,5},{5,6},{6,7},{7,0},{8,9},{9,10},{10,1... | collective-permute-start | bytes 6881288 | tf_op jit(solution)/gta,gtb->gab/dot_general | solution.py:19
  511.7 52.9 %collective-permute-start = (bf16[1,1,160,7168]{3,2,1,0:T(8,128)(2,1)}, bf16[1,1,160,7168]{3,2,1,0:T(8,128)(2,1)S(1)}, u32[]{:S(2)}, u32[]{:S(2)}) collective-permute-start(bf16[1,1,160,7168]{3,2,1,0:T(8,128)(2,1)} %get-tuple-element.146), channel_id=6, source_target_pairs={{0,7},{1,0},{2,1},{3,2},{4,3},{5,4},{6,5},{7,6},{8,15},{9,8},{10,9... | collective-permute-start | bytes 6881288 | tf_op jit(solution)/gta,gtb->gab/dot_general | solution.py:19
  515.3 53.0 %collective-permute-start.2 = (bf16[1,1,160,7168]{3,2,1,0:T(8,128)(2,1)}, bf16[1,1,160,7168]{3,2,1,0:T(8,128)(2,1)}, u32[]{:S(2)}, u32[]{:S(2)}) collective-permute-start(bf16[1,1,160,7168]{3,2,1,0:T(8,128)(2,1)} %get-tuple-element.148), channel_id=7, source_target_pairs={{0,1},{1,2},{2,3},{3,4},{4,5},{5,6},{6,7},{7,0},{8,9},{9,10},{10,1... | collective-permute-start | bytes 6881288 | tf_op jit(solution)/gta,gtb->gab/dot_general | solution.py:19
  564.7 104.6 %collective-permute-start.1 = (bf16[1,1,160,7168]{3,2,1,0:T(8,128)(2,1)S(1)}, bf16[1,1,160,7168]{3,2,1,0:T(8,128)(2,1)}, u32[]{:S(2)}, u32[]{:S(2)}) collective-permute-start(bf16[1,1,160,7168]{3,2,1,0:T(8,128)(2,1)S(1)} %collective-permute-done), channel_id=8, source_target_pairs={{0,7},{1,0},{2,1},{3,2},{4,3},{5,4},{6,5},{7,6},{8,15},{9,8},{10,9... | collective-permute-start | bytes 6881288 | tf_op jit(solution)/gta,gtb->gab/dot_general | solution.py:19
  568.4 100.9 %collective-permute-start.3 = (bf16[1,1,160,7168]{3,2,1,0:T(8,128)(2,1)}, bf16[1,1,160,7168]{3,2,1,0:T(8,128)(2,1)}, u32[]{:S(2)}, u32[]{:S(2)}) collective-permute-start(bf16[1,1,160,7168]{3,2,1,0:T(8,128)(2,1)} %collective-permute-done.2), channel_id=9, source_target_pairs={{0,1},{1,2},{2,3},{3,4},{4,5},{5,6},{6,7},{7,0},{8,9},{9,10},{10,1... | collective-permute-start | bytes 6881288 | tf_op jit(solution)/gta,gtb->gab/dot_general | solution.py:19
  748.3 96.8 %collective-permute-start.4 = (bf16[1,1,160,7168]{3,2,1,0:T(8,128)(2,1)}, bf16[1,1,160,7168]{3,2,1,0:T(8,128)(2,1)S(1)}, u32[]{:S(2)}, u32[]{:S(2)}) collective-permute-start(bf16[1,1,160,7168]{3,2,1,0:T(8,128)(2,1)} %get-tuple-element.179), channel_id=12, source_target_pairs={{0,7},{1,0},{2,1},{3,2},{4,3},{5,4},{6,5},{7,6},{8,15},{9,8},{10,9... | collective-permute-start | bytes 6881288 | tf_op jit(solution)/gta,gtb->gab/dot_general | solution.py:19
  751.9 98.8 %collective-permute-start.6 = (bf16[1,1,160,7168]{3,2,1,0:T(8,128)(2,1)}, bf16[1,1,160,7168]{3,2,1,0:T(8,128)(2,1)}, u32[]{:S(2)}, u32[]{:S(2)}) collective-permute-start(bf16[1,1,160,7168]{3,2,1,0:T(8,128)(2,1)} %get-tuple-element.181), channel_id=13, source_target_pairs={{0,1},{1,2},{2,3},{3,4},{4,5},{5,6},{6,7},{7,0},{8,9},{9,10},{10,1... | collective-permute-start | bytes 6881288 | tf_op jit(solution)/gta,gtb->gab/dot_general | solution.py:19
  845.1 101.8 %collective-permute-start.5 = (bf16[1,1,160,7168]{3,2,1,0:T(8,128)(2,1)S(1)}, bf16[1,1,160,7168]{3,2,1,0:T(8,128)(2,1)S(1)}, u32[]{:S(2)}, u32[]{:S(2)}) collective-permute-start(bf16[1,1,160,7168]{3,2,1,0:T(8,128)(2,1)S(1)} %collective-permute-done.4), channel_id=14, source_target_pairs={{0,7},{1,0},{2,1},{3,2},{4,3},{5,4},{6,5},{7,6},{8,15},{9,8},{10,9... | collective-permute-start | bytes 6881288 | tf_op jit(solution)/gta,gtb->gab/dot_general | solution.py:19
  850.7 100.3 %collective-permute-start.7 = (bf16[1,1,160,7168]{3,2,1,0:T(8,128)(2,1)}, bf16[1,1,160,7168]{3,2,1,0:T(8,128)(2,1)}, u32[]{:S(2)}, u32[]{:S(2)}) collective-permute-start(bf16[1,1,160,7168]{3,2,1,0:T(8,128)(2,1)} %collective-permute-done.6), channel_id=15, source_target_pairs={{0,1},{1,2},{2,3},{3,4},{4,5},{5,6},{6,7},{7,0},{8,9},{9,10},{10,1... | collective-permute-start | bytes 6881288 | tf_op jit(solution)/gta,gtb->gab/dot_general | solution.py:19
  946.9 4.2 copy-start
  951.0 100.0 %collective-permute-start.4 = (bf16[1,1,160,7168]{3,2,1,0:T(8,128)(2,1)}, bf16[1,1,160,7168]{3,2,1,0:T(8,128)(2,1)S(1)}, u32[]{:S(2)}, u32[]{:S(2)}) collective-permute-start(bf16[1,1,160,7168]{3,2,1,0:T(8,128)(2,1)} %get-tuple-element.179), channel_id=12, source_target_pairs={{0,7},{1,0},{2,1},{3,2},{4,3},{5,4},{6,5},{7,6},{8,15},{9,8},{10,9... | collective-permute-start | bytes 6881288 | tf_op jit(solution)/gta,gtb->gab/dot_general | solution.py:19
  952.0 102.7 %collective-permute-start.6 = (bf16[1,1,160,7168]{3,2,1,0:T(8,128)(2,1)}, bf16[1,1,160,7168]{3,2,1,0:T(8,128)(2,1)}, u32[]{:S(2)}, u32[]{:S(2)}) collective-permute-start(bf16[1,1,160,7168]{3,2,1,0:T(8,128)(2,1)} %get-tuple-element.181), channel_id=13, source_target_pairs={{0,1},{1,2},{2,3},{3,4},{4,5},{5,6},{6,7},{7,0},{8,9},{9,10},{10,1... | collective-permute-start | bytes 6881288 | tf_op jit(solution)/gta,gtb->gab/dot_general | solution.py:19
  1051.0 104.6 %collective-permute-start.5 = (bf16[1,1,160,7168]{3,2,1,0:T(8,128)(2,1)S(1)}, bf16[1,1,160,7168]{3,2,1,0:T(8,128)(2,1)S(1)}, u32[]{:S(2)}, u32[]{:S(2)}) collective-permute-start(bf16[1,1,160,7168]{3,2,1,0:T(8,128)(2,1)S(1)} %collective-permute-done.4), channel_id=14, source_target_pairs={{0,7},{1,0},{2,1},{3,2},{4,3},{5,4},{6,5},{7,6},{8,15},{9,8},{10,9... | collective-permute-start | bytes 6881288 | tf_op jit(solution)/gta,gtb->gab/dot_general | solution.py:19
  1054.7 100.9 %collective-permute-start.7 = (bf16[1,1,160,7168]{3,2,1,0:T(8,128)(2,1)}, bf16[1,1,160,7168]{3,2,1,0:T(8,128)(2,1)}, u32[]{:S(2)}, u32[]{:S(2)}) collective-permute-start(bf16[1,1,160,7168]{3,2,1,0:T(8,128)(2,1)} %collective-permute-done.6), channel_id=15, source_target_pairs={{0,1},{1,2},{2,3},{3,4},{4,5},{5,6},{6,7},{7,0},{8,9},{9,10},{10,1... | collective-permute-start | bytes 6881288 | tf_op jit(solution)/gta,gtb->gab/dot_general | solution.py:19
  1155.6 1.4 copy-start
Sparse Core Ops, SparseCore 0:
  13.8 204.4 all-gather.4
  748.1 346.4 reduce-scatter.3
where the time goes:
time: 1220 us; the launch traced here: 1210 us
  matrix products  682 us (56%)
  waiting for transfers between devices  345 us (28%)
  local copies, waits for them, and re-layouts  88.9 us (7%)
  other arithmetic  49.9 us (4%)
  starting transfers between devices  27 us (2%)
  between operations  14.5 us (1%)
    dot_general x8, matrix products, by_group(): jnp.einsum('gta,gtb->gab', a, b, preferred_element_type=jnp.float32)  516 us
    unnamed x4, waiting for transfers between devices  201 us
    dot_general x18, waiting for transfers between devices, by_group(): jnp.einsum('gta,gtb->gab', a, b, preferred_element_type=jnp.float32)  143 us
    dot_general x1, matrix products, step(): d_hidden = jnp.dot(dy, w_down.T, preferred_element_type=jnp.float32)  90.6 us
    dot_general x5, local copies, waits for them, and re-layouts, by_group(): jnp.einsum('gta,gtb->gab', a, b, preferred_element_type=jnp.float32)  81 us
    dot_general x1, matrix products, step(): dx = jnp.dot(d_pre, w_in.T)  75.5 us
    reshape x1, other arithmetic, by_group(): return product.astype(jnp.bfloat16).reshape(-1, b.shape[-1])  49.9 us
    dot_general x18, starting transfers between devices, by_group(): jnp.einsum('gta,gtb->gab', a, b, preferred_element_type=jnp.float32)  26.9 us
  transfers between devices with their start and end apart: 20, of which 8 were waited for; matrix products, arithmetic and copies ran while one was open for 67% of the time, Pallas kernels for 0%

commit v1 on v0

v1 whole, which is shorter than its diff:
```python
import functools

import jax
import jax.numpy as jnp
from jax import lax
from jax.experimental import pallas as pl
from jax.experimental.pallas import tpu as pltpu
from jax.sharding import PartitionSpec as P

F32, BF16 = jnp.float32, jnp.bfloat16
NT = (((1,), (1,)), ((), ()))
TN = (((0,), (0,)), ((), ()))
G = 7
STRIP = 16
SLOTS = 4
VMEM = 67043328
PIECES = 3
C0 = 0.7978845608028654
C1 = 0.044715


def gather_reduce_kernel(
    dy, pre, w_in, w_down, dy_all, d_pre, hidden, dx,
    dyv, ring, dpre, hid, preb, held, precv, psend, crecv, cs,
    acc, ws, ios, prs, ls, lr, ps, pr, pss, psr, css, csr, credit,
):
    R, D = dy.shape
    F = pre.shape[1]
    CH, T = D // G, F // G
    t = lax.axis_index("tp")
    z, c = t // 2, t % 2
    partner = t + 1 - 2 * c

    def rows(s, core):
        return pl.ds(pl.multiple_of((2 * s + core) * R, R), R)

    def chunk(q):
        return pl.ds(pl.multiple_of(q * CH, CH), CH)

    def tile(j):
        return pl.ds(pl.multiple_of(j * T, T), T)

    def remote(src, dst, send, recv, to):
        return pltpu.make_async_remote_copy(
            src_ref=src, dst_ref=dst, send_sem=send, recv_sem=recv,
            device_id={"tp": to}, device_id_type=pl.DeviceIdType.MESH,
        )

    def line(way, hop, s, q, own=False):
        here = dy_all.at[rows(s, c), chunk(q)]
        src = dy.at[:, chunk(q)] if own else here
        return remote(src, here, ls.at[way, hop, q], lr.at[s, q], t + 2 - 4 * way)

    def across(s, q, own=False):
        here = dy_all.at[rows(s, c), chunk(q)]
        src = dy.at[:, chunk(q)] if own else here
        return remote(src, here, ps.at[s, q], pr.at[s, q], partner)

    def gather_step(k, q):
        hop = k + 1

        @pl.when(z >= hop)
        def _():
            line(0, hop, z - hop, q).wait_recv()

            @pl.when(z < 3)
            def _():
                line(0, hop, z - hop, q).start()

            across(z - hop, q).start()

        @pl.when(z + hop <= 3)
        def _():
            line(1, hop, z + hop, q).wait_recv()

            @pl.when(z > 0)
            def _():
                line(1, hop, z + hop, q).start()

            across(z + hop, q).start()

    def pair(k, g):
        return remote(
            psend.at[:, chunk(g)], precv.at[k % 2, :, chunk(g)], pss.at[g], psr.at[k % 2, g], partner
        )

    def chain(way, a, g):
        return remote(
            cs.at[way, :, chunk(g)], crecv.at[way, (a - 1) % 2, :, chunk(g)],
            css.at[way, g], csr.at[way, (a - 1) % 2, g], t + 2 - 4 * way,
        )

    def strips(step):
        @pl.loop(0, R // STRIP)
        def _(i):
            step(pl.ds(pl.multiple_of(i * STRIP, STRIP), STRIP))

    def pair_add(k, s, g):
        pair(k, g).wait_recv()
        source = jnp.logical_and(z % 3 == 0, k > 0)
        way = z // 3

        @pl.when(source)
        def _():
            @pl.when(k >= 2)
            def _():
                chain(way, k, g).wait_send()

            @pl.when(jnp.logical_and(k == 3, g == 0))
            def _():
                pl.semaphore_wait(credit, 1)

            def step(r):
                total = held[s, r, chunk(g)] + precv[k % 2, r, chunk(g)].astype(F32)
                cs[way, r, chunk(g)] = total.astype(BF16)

            strips(step)
            chain(way, k, g).start()

        @pl.when(jnp.logical_not(source))
        def _():
            def step(r):
                held[s, r, chunk(g)] += precv[k % 2, r, chunk(g)].astype(F32)

            strips(step)

    def arrive(way, a, g, forward, sent_before):
        d = a + way * (3 - 2 * a)
        chain(way, a, g).wait_recv()
        old = (a - 1) % 2

        @pl.when(forward)
        def _():
            @pl.when(sent_before)
            def _():
                chain(way, a, g).wait_send()

            def step(r):
                total = held[d, r, chunk(g)] + crecv[way, old, r, chunk(g)].astype(F32)
                cs[way, r, chunk(g)] = total.astype(BF16)

            strips(step)
            chain(way, a, g).start()

        @pl.when(jnp.logical_not(forward))
        def _():
            def step(r):
                held[d, r, chunk(g)] += crecv[way, old, r, chunk(g)].astype(F32)

            strips(step)

    middle = jnp.logical_and(z >= 1, z <= 2)

    H = T // 2

    def load(src, lo, n, slot, part):
        return pltpu.make_async_copy(
            src, ring.at[slot, pl.ds(part * H, H), :], ws.at[slot, part]
        )

    def fetch(n):
        i, slot = n % 28, n % SLOTS

        @pl.when(n < 112)
        def _():
            for part in range(2):

                @pl.when(i < 14)
                def _():
                    src = w_down.at[
                        pl.ds(pl.multiple_of((i // 2) * T + part * H, H), H),
                        pl.ds(pl.multiple_of((i % 2) * F, F), F),
                    ]
                    load(src, 0, n, slot, part).start()

                @pl.when(i >= 14)
                def _():
                    src = w_in.at[pl.ds(pl.multiple_of((i - 14) * T + part * H, H), H), :]
                    load(src, 0, n, slot, part).start()

    def ready(n):
        slot = n % SLOTS
        for part in range(2):
            load(w_in.at[pl.ds(0, H), :], 0, n, slot, part).wait()
        return slot

    def pre_copies(s, m):
        return [
            pltpu.make_async_copy(
                pre.at[rows(s, core), tile(m)], preb.at[m % 2, pl.ds(i * R, R), :], prs.at[m % 2, i]
            )
            for i, core in enumerate((c, 1 - c))
        ]

    def out_copies(s):
        return [
            pltpu.make_async_copy(v.at[pl.ds(i * R, R), :], o.at[rows(s, core), :], ios.at[2 + 2 * j + i])
            for j, (v, o) in enumerate(((dpre, d_pre), (hid, hidden)))
            for i, core in enumerate((c, 1 - c))
        ]

    barrier = pltpu.get_barrier_semaphore()
    pl.semaphore_signal(barrier, inc=1, device_id={"tp": partner}, device_id_type=pl.DeviceIdType.MESH)

    @pl.when(z > 0)
    def _():
        pl.semaphore_signal(barrier, inc=1, device_id={"tp": t - 2}, device_id_type=pl.DeviceIdType.MESH)

    @pl.when(z < 3)
    def _():
        pl.semaphore_signal(barrier, inc=1, device_id={"tp": t + 2}, device_id_type=pl.DeviceIdType.MESH)

    for n in range(SLOTS - 1):
        fetch(jnp.int32(n))

    @pl.when(middle)
    def _():
        pl.semaphore_wait(barrier, 3)

    @pl.when(jnp.logical_not(middle))
    def _():
        pl.semaphore_wait(barrier, 2)

    @pl.loop(0, G)
    def _(q):
        @pl.when(z < 3)
        def _():
            line(0, 0, z, q, own=True).start()

        @pl.when(z > 0)
        def _():
            line(1, 0, z, q, own=True).start()

        across(z, q, own=True).start()

    mirror = z // 2
    u = z + mirror * (3 - 2 * z)

    @pl.loop(0, 4)
    def _(k):
        base = (k // 2) * k + (1 - k // 2) * ((k + u) % 2)
        s = base + mirror * (3 - 2 * base)

        for cp in pre_copies(s, 0):
            cp.start()

        @pl.when(k == 0)
        def _():
            pltpu.make_async_copy(dy, dyv.at[pl.ds(0, R), :], ios.at[0]).start()

        @pl.when(k > 0)
        def _():
            pltpu.make_async_copy(dy_all.at[rows(s, c), :], dyv.at[pl.ds(0, R), :], ios.at[0]).start()

        @pl.loop(0, G)
        def _(q):
            across(s, q).wait_recv()

        other = pltpu.make_async_copy(dy_all.at[rows(s, 1 - c), :], dyv.at[pl.ds(R, R), :], ios.at[1])
        other.start()
        pltpu.make_async_copy(dy, dyv.at[pl.ds(0, R), :], ios.at[0]).wait()

        keep = pltpu.make_async_copy(dyv.at[pl.ds(0, R), :], dy_all.at[rows(s, c), :], ios.at[0])

        @pl.when(k == 0)
        def _():
            keep.start()

        other.wait()

        @pl.loop(0, G)
        def _(m):
            n = 28 * k + 2 * m
            fetch(n + SLOTS - 1)
            slot = ready(n)
            acc[...] = lax.dot_general(dyv[:, :F], ring[slot], NT, preferred_element_type=F32)
            fetch(n + SLOTS)
            slot = ready(n + 1)
            acc[...] += lax.dot_general(dyv[:, F:], ring[slot], NT, preferred_element_type=F32)

            @pl.when(m < G - 1)
            def _():
                for cp in pre_copies(s, m + 1):
                    cp.start()

            for cp in pre_copies(s, m):
                cp.wait()

            @pl.loop(0, 2 * R // STRIP)
            def _(i):
                strip = pl.ds(pl.multiple_of(i * STRIP, STRIP), STRIP)
                v = preb[m % 2, strip, :].astype(F32)
                sq = v * v
                th = jnp.tanh((C0 * v) * (1.0 + C1 * sq))
                cdf = 0.5 + 0.5 * th
                slope = cdf + (v * (1.0 - th * th)) * (0.5 * C0) * (1.0 + (3 * C1) * sq)
                dpre[strip, tile(m)] = (acc[strip, :] * slope).astype(BF16)
                hid[strip, tile(m)] = (v * cdf).astype(BF16)

            @pl.when(jnp.logical_and(k < 3, m % 2 == 1))
            def _():
                gather_step(k, m // 2)

            @pl.when(jnp.logical_and(k >= 2, middle))
            def _():
                arrive(z - 1, k - 1, m, k == 3, False)

        @pl.when(jnp.logical_and(k == 2, middle))
        def _():
            pl.semaphore_signal(
                credit, inc=1, device_id={"tp": t - 2 + 4 * (z - 1)}, device_id_type=pl.DeviceIdType.MESH
            )

        @pl.when(k == 0)
        def _():
            keep.wait()

        for cp in out_copies(s):
            cp.start()

        @pl.loop(0, G)
        def _(m):
            for half in range(2):
                n = 28 * k + 14 + 2 * m + half
                fetch(n + SLOTS - 1)
                slot = ready(n)
                term = lax.dot_general(dpre[...], ring[slot], NT, preferred_element_type=F32)
                held[s, :, tile(2 * m + half)] = term[:R]
                psend[:, tile(2 * m + half)] = term[R:].astype(BF16)
            pair(k, m).start()

            @pl.when(jnp.logical_and(k < 3, m % 2 == 0))
            def _():
                gather_step(k, 3 + m // 2)

            @pl.when(jnp.logical_and(k == 3, middle))
            def _():
                arrive(2 - z, 2, m, False, False)

            @pl.when(m > 0)
            def _():
                pair_add(k, s, m - 1)

        pair_add(k, s, G - 1)

        @pl.loop(0, G)
        def _(m):
            pair(k, m).wait_send()

        for cp in out_copies(s):
            cp.wait()

    @pl.loop(0, G + 1)
    def _(g):
        @pl.when(jnp.logical_and(g < G, middle))
        def _():
            arrive(z - 1, 3, g, True, True)

        @pl.when(jnp.logical_and(g > 0, middle))
        def _():
            arrive(2 - z, 3, g - 1, True, False)

        @pl.when(jnp.logical_and(g < G, jnp.logical_not(middle)))
        def _():
            arrive((3 - z) // 3, 3, g, False, False)

    @pl.loop(0, G)
    def _(g):
        def step(r):
            psend[r, chunk(g)] = held[z, r, chunk(g)].astype(BF16)

        strips(step)

    out = pltpu.make_async_copy(psend, dx, ios.at[0])
    out.start()

    @pl.loop(0, G)
    def _(q):
        @pl.when(middle)
        def _():
            chain(0, 3, q).wait_send()
            chain(1, 3, q).wait_send()

        @pl.when(jnp.logical_not(middle))
        def _():
            chain(z // 3, 3, q).wait_send()

        for hop in range(3):

            @pl.when(jnp.logical_and(z >= hop, z < 3))
            def _():
                line(0, hop, z, q).wait_send()

            @pl.when(jnp.logical_and(z + hop <= 3, z > 0))
            def _():
                line(1, hop, z, q).wait_send()

        for s in range(4):
            across(s, q).wait_send()

    out.wait()


def gather_reduce(dy, pre, w_in, w_down):
    R, D = dy.shape
    rows, F = pre.shape
    T = F // G
    dma = pltpu.SemaphoreType.DMA
    any_spec = pl.BlockSpec(memory_space=pl.ANY)
    return pl.pallas_call(
        gather_reduce_kernel,
        name="gather_reduce",
        out_shape=(
            jax.ShapeDtypeStruct((rows, D), BF16),
            jax.ShapeDtypeStruct((rows, F), BF16),
            jax.ShapeDtypeStruct((rows, F), BF16),
            jax.ShapeDtypeStruct((R, D), BF16),
        ),
        in_specs=[any_spec] * 4,
        out_specs=[any_spec] * 4,
        scratch_shapes=[
            pltpu.VMEM((2 * R, D), BF16),
            pltpu.VMEM((SLOTS, T, F), BF16),
            pltpu.VMEM((2 * R, F), BF16),
            pltpu.VMEM((2 * R, F), BF16),
            pltpu.VMEM((2, 2 * R, T), BF16),
            pltpu.VMEM((4, R, D), F32),
            pltpu.VMEM((2, R, D), BF16),
            pltpu.VMEM((R, D), BF16),
            pltpu.VMEM((2, 2, R, D), BF16),
            pltpu.VMEM((2, R, D), BF16),
            pltpu.VMEM((2 * R, T), F32),
            dma((SLOTS, 2)),
            dma((6,)),
            dma((2, 2)),
            dma((2, 3, G)),
            dma((4, G)),
            dma((4, G)),
            dma((4, G)),
            dma((G,)),
            dma((2, G)),
            dma((2, G)),
            dma((2, 2, G)),
            pltpu.SemaphoreType.REGULAR,
        ],
        compiler_params=pltpu.CompilerParams(
            collective_id=0, has_side_effects=True, vmem_limit_bytes=VMEM
        ),
        cost_estimate=pl.CostEstimate(
            flops=4 * rows * D * F, bytes_accessed=16 * D * F, transcendentals=rows * F
        ),
    )(dy, pre, w_in, w_down)


def weight_grad_kernel(a, b, *rest):
    o = rest[-1]
    o[...] = lax.dot_general(a[...], b[...], TN, preferred_element_type=F32).astype(BF16)


def weight_grad(a, b, total, start, into, bm, bn):
    rows, A = a.shape
    B = b.shape[1]
    off = start // bm
    return pl.pallas_call(
        weight_grad_kernel,
        name="weight_grad",
        grid=(B // bn, A // bm),
        out_shape=jax.ShapeDtypeStruct((total, B), BF16),
        in_specs=[
            pl.BlockSpec((rows, bm), lambda j, i: (0, i)),
            pl.BlockSpec((rows, bn), lambda j, i: (0, j)),
        ]
        + ([] if into is None else [pl.BlockSpec(memory_space=pl.ANY)]),
        out_specs=pl.BlockSpec((bm, bn), lambda j, i: (i + off, j)),
        input_output_aliases={} if into is None else {2: 0},
        compiler_params=pltpu.CompilerParams(
            dimension_semantics=("arbitrary", "arbitrary"), vmem_limit_bytes=VMEM
        ),
        cost_estimate=pl.CostEstimate(
            flops=2 * rows * A * B, bytes_accessed=2 * (rows * (A + B) + A * B), transcendentals=0
        ),
    )(a, b, *([] if into is None else [into]))


CUTS = (0, 2304, 4608, 7168)


def solution(mesh):
    def body(x, dy, pre, w_in, w_down):
        dy_all, d_pre, hidden, dx = gather_reduce(dy, pre, w_in, w_down)
        x_late, d_pre = lax.optimization_barrier((x, d_pre))
        D, F = w_in.shape
        dw_down = weight_grad(hidden, dy_all, F, 0, None, 896, 1792)
        dw_in = None
        for lo, hi in zip(CUTS[:-1], CUTS[1:]):
            piece = lax.all_gather(x_late[:, lo:hi], "tp", axis=0, tiled=True)
            dw_in = weight_grad(piece, d_pre, D, lo, dw_in, 256, 3584)
        return dx, dw_in, dw_down

    rows = P(("dp", "tp"), None)
    return jax.shard_map(
        body,
        mesh=mesh,
        in_specs=(rows, rows, P("dp", "tp"), P(None, "tp"), P("tp", None)),
        out_specs=(rows, P("dp", "tp"), P(("dp", "tp"), None)),
        check_vma=False,
    )
```

time: 1220 us -> 524 us (0.43)
  matrix products: 682 us -> 0 us
  Pallas kernels: 0 us -> 445 us
  waiting for transfers between devices: 345 us -> 57.4 us
  local copies, waits for them, and re-layouts: 88.9 us -> 7.8 us
  other arithmetic: 49.9 us -> 0 us
  starting transfers between devices: 27 us -> 0.3 us
    dot_general x10 -> x0, matrix products: 682 us -> none  [the longest x8 516 us: by_group(): jnp.einsum('gta,gtb->gab', a, b, preferred_element_type=jnp.float32)]
    pallas_call x0 -> x5, Pallas kernels: none -> 445 us  [the longest x1 282 us: gather_reduce(): pl.pallas_call(gather_reduce_kernel, name='gather_reduce', out_shape=(jax...]
    unnamed x4 -> x3, waiting for transfers between devices: 201 us -> 0.73 us
    dot_general x18 -> x0, waiting for transfers between devices: 143 us -> none  [by_group(): jnp.einsum('gta,gtb->gab', a, b, preferred_element_type=jnp.float32)]
    dot_general x9 -> x0, local copies, waits for them, and re-layouts: 82.5 us -> none  [the longest x5 81 us: by_group(): jnp.einsum('gta,gtb->gab', a, b, preferred_element_type=jnp.float32)]
    all_gather x0 -> x3, waiting for transfers between devices: none -> 56.7 us  [body(): piece = lax.all_gather(x_late[:, lo:hi], 'tp', axis=0, tiled=True)]
    reshape x1 -> x0, other arithmetic: 49.9 us -> none  [by_group(): return product.astype(jnp.bfloat16).reshape(-1, b.shape[-1])]
    dot_general x18 -> x0, starting transfers between devices: 26.9 us -> none  [by_group(): jnp.einsum('gta,gtb->gab', a, b, preferred_element_type=jnp.float32)]
  transfers between devices with their start and end apart: 20 -> 3, of which waited for: 8 -> 2; matrix products, arithmetic and copies ran while one was open for 67% -> 0% of each run, Pallas kernels for 0% -> 25%
where the time goes in v1:
time: 524 us
  Pallas kernels  445 us (85%)
  waiting for transfers between devices  57.4 us (11%)
  between operations  13.8 us (3%)
  local copies, waits for them, and re-layouts  7.8 us (1%)
    pallas_call x1, Pallas kernels, gather_reduce(): pl.pallas_call(gather_reduce_kernel, name='gather_reduce', out_shape=(jax...  282 us
    pallas_call x4, Pallas kernels, weight_grad(): pl.pallas_call(weight_grad_kernel, name='weight_grad', grid=(B // bn, A /...  162 us
    all_gather x3, waiting for transfers between devices, body(): piece = lax.all_gather(x_late[:, lo:hi], 'tp', axis=0, tiled=True)  56.7 us
  transfers between devices with their start and end apart: 3, of which 2 were waited for; matrix products, arithmetic and copies ran while one was open for 0% of the time, Pallas kernels for 25%

profile of v1, /device:TPU:0, one launch (start us, length us, event | category | flops | bytes accessed | tf_op | source)
XLA Modules:
  0.0 524.0 jit_solution(272893101569101555)
XLA Ops:
  7.2 0.0 all-gather.8.cloned.1.call-start
  7.2 282.3 %gather_reduce.1 = (bf16[1280,7168]{1,0:T(8,128)(2,1)}, bf16[1280,3584]{1,0:T(8,128)(2,1)}, bf16[1280,3584]{1,0:T(8,128)(2,1)}, bf16[160,7168]{1,0:T(8,128)(2,1)}) custom-call(bf16[160,7168]{1,0:T(8,128)(2,1)} %dy.1, bf16[1280,3584]{1,0:T(8,128)(2,1)} %pre.1, bf16[7168,3584]{1,0:T(8,128)(2,1)} %w_in.1, bf16[3584,7168]{1,0:T(8,128)(2,1)} %w_down.1), custom_call_target="tpu_custom_call" | custom-call | flops 131533373440 | bytes 411041792 | tf_op jit(solution)/shard_map/gather_reduce/pallas_call | solution.py:410
  289.5 2.5 fusion
  292.1 0.0 all-gather.8.cloned.1.call-update
  292.1 0.0 all-gather.6.cloned.1.call-start
  292.1 0.7 all-gather.6.cloned.1.call-update
  292.8 0.2 all-gather.4.cloned.1.call-start
  293.1 2.1 slice.9
  295.2 0.0 all-gather.4.cloned.1.call-update
  295.2 74.9 %weight_grad.7 = bf16[3584,7168]{1,0:T(8,128)(2,1)} custom-call(bf16[1280,3584]{1,0:T(8,128)(2,1)} %get-tuple-element.13.a, bf16[1280,7168]{1,0:T(8,128)(2,1)} %get-tuple-element.14.b), custom_call_target="tpu_custom_call" | custom-call | flops 65766686720 | bytes 78905344 | tf_op jit(solution)/shard_map/weight_grad/pallas_call | solution.py:464
  370.1 0.0 all-gather.8.cloned.1.call-done.a
  370.1 28.4 %weight_grad.4.rest_0_ = bf16[7168,3584]{1,0:T(8,128)(2,1)} custom-call(bf16[1280,2304]{1,0:T(8,128)(2,1)} %all-gather.8.cloned.1.call-done.a, bf16[1280,3584]{1,0:T(8,128)(2,1)} %get-tuple-element.12.b), custom_call_target="tpu_custom_call" | custom-call | flops 21139292160 | bytes 31588352 | tf_op jit(solution)/shard_map/weight_grad/pallas_call | solution.py:464
  398.5 17.2 %all-gather.6.cloned.1.call-done.a = bf16[1280,2304]{1,0:T(8,128)(2,1)} async-done(((bf16[160,2304]{1,0:T(8,128)(2,1)}), bf16[1280,2304]{1,0:T(8,128)(2,1)}) %all-gather.6.cloned.1.call-update) | async-done | bytes 5898256 | tf_op jit(solution)/shard_map/all_gather | solution.py:496
  415.6 28.3 %weight_grad.5.rest_0_ = bf16[7168,3584]{1,0:T(8,128)(2,1)} custom-call(bf16[1280,2304]{1,0:T(8,128)(2,1)} %all-gather.6.cloned.1.call-done.a, bf16[1280,3584]{1,0:T(8,128)(2,1)} %get-tuple-element.12.b, bf16[7168,3584]{1,0:T(8,128)(2,1)} %weight_grad.4.rest_0_), custom_call_target="tpu_custom_call", output_to_operand_aliasing={{}: (2, {})} | custom-call | flops 21139292160 | bytes 31588352 | tf_op jit(solution)/shard_map/weight_grad/pallas_call | solution.py:464
  443.9 39.5 %all-gather.4.cloned.1.call-done.a = bf16[1280,2560]{1,0:T(8,128)(2,1)} async-done(((bf16[160,2560]{1,0:T(8,128)(2,1)}), bf16[1280,2560]{1,0:T(8,128)(2,1)}) %all-gather.4.cloned.1.call-update) | async-done | bytes 6553616 | tf_op jit(solution)/shard_map/all_gather | solution.py:496
  483.4 30.9 %weight_grad.6 = bf16[7168,3584]{1,0:T(8,128)(2,1)} custom-call(bf16[1280,2560]{1,0:T(8,128)(2,1)} %all-gather.4.cloned.1.call-done.a, bf16[1280,3584]{1,0:T(8,128)(2,1)} %get-tuple-element.12.b, bf16[7168,3584]{1,0:T(8,128)(2,1)} %weight_grad.5.rest_0_), custom_call_target="tpu_custom_call", output_to_operand_aliasing={{}: (2, {})} | custom-call | flops 23488102400 | bytes 34078720 | tf_op jit(solution)/shard_map/weight_grad/pallas_call | solution.py:464
  514.3 3.2 copy.13
Async XLA Ops:
  7.2 362.9 %all-gather.8.cloned.1.call-start = ((), (), s32[]{:S(2)}) async-start(), calls=%async_computation.2 | async-start | bytes 6635520 | tf_op jit(solution)/shard_map/all_gather | solution.py:496
  292.1 123.5 %all-gather.6.cloned.1.call-start = ((), (), s32[]{:S(2)}) async-start(), calls=%async_computation.1 | async-start | bytes 6635520 | tf_op jit(solution)/shard_map/all_gather | solution.py:496
  292.8 190.6 %all-gather.4.cloned.1.call-start = ((), (), s32[]{:S(2)}) async-start(), calls=%async_computation | async-start | bytes 7372800 | tf_op jit(solution)/shard_map/all_gather | solution.py:496
Sparse Core Ops, SparseCore 0:
  292.2 61.5 all-gather.7
  355.5 60.1 all-gather.5
  417.8 65.5 all-gather.3

commit v2 on v1

v2 whole, which is shorter than its diff:
```python
import functools

import jax
import jax.numpy as jnp
from jax import lax
from jax.experimental import pallas as pl
from jax.experimental.pallas import tpu as pltpu
from jax.sharding import PartitionSpec as P

F32, BF16 = jnp.float32, jnp.bfloat16
NT = (((1,), (1,)), ((), ()))
TN = (((0,), (0,)), ((), ()))
G = 7
STRIP = 16
SLOTS = 5
VMEM = 67043328
XG = 4
GC = 14
XL = 2560
XW = 2048
C0 = 0.7978845608028654
C1 = 0.044715


def gather_reduce_kernel(
    x, dy, pre, w_in, w_down, dy_all, d_pre, hidden, dx, x_part, slopes, x_late0, x_late1,
    dyv, ring, dpre, slp, held, precv, psend, crecv, cs,
    acc, ws, ios, els, prs, ls, lr, ps, pr, xls, xlr, xps, xpr, pss, psr, css, csr, credit,
):
    R, D = dy.shape
    F = pre.shape[1]
    CH, T = D // G, F // G
    XC = x_part.shape[1] // XG
    t = lax.axis_index("tp")
    z, c = t // 2, t % 2
    partner = t + 1 - 2 * c

    def rows(s, core):
        return pl.ds(pl.multiple_of((2 * s + core) * R, R), R)

    def chunk(q):
        return pl.ds(pl.multiple_of(q * CH, CH), CH)

    def slab(q):
        return pl.ds(pl.multiple_of(q * (D // GC), D // GC), D // GC)

    def tile(j):
        return pl.ds(pl.multiple_of(j * T, T), T)

    def remote(src, dst, send, recv, to):
        return pltpu.make_async_remote_copy(
            src_ref=src, dst_ref=dst, send_sem=send, recv_sem=recv,
            device_id={"tp": to}, device_id_type=pl.DeviceIdType.MESH,
        )

    def line(way, hop, s, q, own=False):
        here = dy_all.at[rows(s, c), chunk(q)]
        src = dy.at[:, chunk(q)] if own else here
        return remote(src, here, ls.at[way, hop, q], lr.at[s, q], t + 2 - 4 * way)

    def across(s, q, own=False):
        here = dy_all.at[rows(s, c), chunk(q)]
        src = dy.at[:, chunk(q)] if own else here
        return remote(src, here, ps.at[s, q], pr.at[s, q], partner)

    def xcols(q):
        return pl.ds(pl.multiple_of(q * XC, XC), XC)

    def x_line(way, hop, s, q, own=False):
        here = x_part.at[rows(s, c), xcols(q)]
        src = x.at[:, xcols(q)] if own else here
        return remote(src, here, xls.at[way, hop, q], xlr.at[s, q], t + 2 - 4 * way)

    def x_across(s, q, own=False):
        here = x_part.at[rows(s, c), xcols(q)]
        src = x.at[:, xcols(q)] if own else here
        return remote(src, here, xps.at[s, q], xpr.at[s, q], partner)

    def send_own(along, over, q):
        @pl.when(z < 3)
        def _():
            along(0, 0, z, q, own=True).start()

        @pl.when(z > 0)
        def _():
            along(1, 0, z, q, own=True).start()

        over(z, q, own=True).start()

    def pass_on(along, over, hop, q):
        @pl.when(z >= hop)
        def _():
            along(0, hop, z - hop, q).wait_recv()

            @pl.when(z < 3)
            def _():
                along(0, hop, z - hop, q).start()

            over(z - hop, q).start()

        @pl.when(z + hop <= 3)
        def _():
            along(1, hop, z + hop, q).wait_recv()

            @pl.when(z > 0)
            def _():
                along(1, hop, z + hop, q).start()

            over(z + hop, q).start()

    def drain(along, over, q):
        for hop in range(3):

            @pl.when(jnp.logical_and(z >= hop, z < 3))
            def _():
                along(0, hop, z, q).wait_send()

            @pl.when(jnp.logical_and(z + hop <= 3, z > 0))
            def _():
                along(1, hop, z, q).wait_send()

        for s in range(4):
            over(s, q).wait_send()

    def pair(k, g):
        return remote(
            psend.at[:, chunk(g)], precv.at[k % 2, :, chunk(g)], pss.at[g], psr.at[k % 2, g], partner
        )

    def chain(way, a, g):
        return remote(
            cs.at[way, :, slab(g)], crecv.at[way, (a - 1) % 2, :, slab(g)],
            css.at[way, g], csr.at[way, (a - 1) % 2, g], t + 2 - 4 * way,
        )

    def strips(step):
        @pl.loop(0, R // STRIP)
        def _(i):
            step(pl.ds(pl.multiple_of(i * STRIP, STRIP), STRIP))

    def pair_add(k, s, g):
        pair(k, g).wait_recv()
        source = jnp.logical_and(z % 3 == 0, k < 3)
        way = z // 3

        @pl.when(source)
        def _():
            @pl.when(jnp.logical_and(k == 2, g == 0))
            def _():
                pl.semaphore_wait(credit, 1)

            @pl.loop(0, GC // G)
            def _(j):
                piece = g * (GC // G) + j

                @pl.when(k >= 1)
                def _():
                    chain(way, k + 1, piece).wait_send()

                def step(r):
                    total = held[s, r, slab(piece)] + precv[k % 2, r, slab(piece)].astype(F32)
                    cs[way, r, slab(piece)] = total.astype(BF16)

                strips(step)
                chain(way, k + 1, piece).start()

        @pl.when(jnp.logical_not(source))
        def _():
            def step(r):
                held[s, r, chunk(g)] += precv[k % 2, r, chunk(g)].astype(F32)

            strips(step)

    def arrive(way, a, g, forward, sent_before):
        d = a + way * (3 - 2 * a)
        chain(way, a, g).wait_recv()
        old = (a - 1) % 2

        @pl.when(forward)
        def _():
            @pl.when(sent_before)
            def _():
                chain(way, a, g).wait_send()

            def step(r):
                total = held[d, r, slab(g)] + crecv[way, old, r, slab(g)].astype(F32)
                cs[way, r, slab(g)] = total.astype(BF16)

            strips(step)
            chain(way, a, g).start()

        @pl.when(jnp.logical_not(forward))
        def _():
            def step(r):
                held[d, r, slab(g)] += crecv[way, old, r, slab(g)].astype(F32)

            strips(step)

    middle = jnp.logical_and(z >= 1, z <= 2)
    ends = z % 3 == 0

    def hooks(k, v):
        @pl.when(jnp.logical_and(k >= 1, middle))
        def _():
            @pl.when(v == 0)
            def _():
                @pl.loop(0, 3)
                def _(g):
                    arrive(z - 1, k, g, k > 1, k == 3)

            @pl.when(v <= 10)
            def _():
                arrive(z - 1, k, v + 3, k > 1, k == 3)

        @pl.when(jnp.logical_and(k == 3, middle))
        def _():
            @pl.when(v < G)
            def _():
                @pl.loop(0, 2)
                def _(j):
                    arrive(2 - z, 2, 2 * v + j, False, False)

            @pl.when(v >= 3)
            def _():
                arrive(2 - z, 3, v - 3, True, False)

    def late(k):
        @pl.when(jnp.logical_and(k == 3, middle))
        def _():
            @pl.loop(GC - 3, GC)
            def _(g):
                arrive(2 - z, 3, g, True, False)

    H = T // 2

    def load(src, lo, n, slot, part):
        return pltpu.make_async_copy(
            src, ring.at[slot, pl.ds(part * H, H), :], ws.at[slot, part]
        )

    def fetch(n):
        i, slot = n % 28, n % SLOTS

        @pl.when(n < 112)
        def _():
            for part in range(2):

                @pl.when(i < 14)
                def _():
                    src = w_down.at[
                        pl.ds(pl.multiple_of((i // 2) * T + part * H, H), H),
                        pl.ds(pl.multiple_of((i % 2) * F, F), F),
                    ]
                    load(src, 0, n, slot, part).start()

                @pl.when(i >= 14)
                def _():
                    src = w_in.at[pl.ds(pl.multiple_of((i - 14) * T + part * H, H), H), :]
                    load(src, 0, n, slot, part).start()

    def ready(n):
        slot = n % SLOTS
        for part in range(2):
            load(w_in.at[pl.ds(0, H), :], 0, n, slot, part).wait()
        return slot

    def slope_copies(s, m):
        return [
            pltpu.make_async_copy(
                slopes.at[rows(s, core), tile(m)], slp.at[m % 2, pl.ds(i * R, R), :], prs.at[m % 2, i]
            )
            for i, core in enumerate((c, 1 - c))
        ]

    def out_copies(s):
        return [
            pltpu.make_async_copy(dpre.at[pl.ds(i * R, R), :], d_pre.at[rows(s, core), :], ios.at[2 + i])
            for i, core in enumerate((c, 1 - c))
        ]

    def e_block(i):
        return pl.ds(pl.multiple_of((i // G) * (2 * R), 2 * R), 2 * R), tile(i % G)

    def e_in(i):
        r, cl = e_block(i)
        return pltpu.make_async_copy(pre.at[r, cl], dpre.at[:, tile(i % 2)], els.at[0, i % 2])

    def e_out(i):
        r, cl = e_block(i)
        return (
            pltpu.make_async_copy(dpre.at[:, tile(2 + i % 2)], hidden.at[r, cl], els.at[1, i % 2]),
            pltpu.make_async_copy(slp.at[i % 2], slopes.at[r, cl], els.at[2, i % 2]),
        )

    def e_step(i):
        @pl.when(i + 1 < 4 * G)
        def _():
            e_in(i + 1).start()

        @pl.when(i >= 2)
        def _():
            for cp in e_out(i - 2):
                cp.wait()

        e_in(i).wait()

        @pl.loop(0, 2 * R // STRIP)
        def _(j):
            strip = pl.ds(pl.multiple_of(j * STRIP, STRIP), STRIP)
            v = dpre[strip, tile(i % 2)].astype(F32)
            sq = v * v
            th = jnp.tanh(v * (C0 + (C0 * C1) * sq))
            cdf = 0.5 + 0.5 * th
            slp[i % 2, strip, :] = cdf + (v * (1.0 - th * th)) * (0.5 * C0 + (1.5 * C0 * C1) * sq)
            dpre[strip, tile(2 + i % 2)] = (v * cdf).astype(BF16)

        for cp in e_out(i):
            cp.start()

    barrier = pltpu.get_barrier_semaphore()
    pl.semaphore_signal(barrier, inc=1, device_id={"tp": partner}, device_id_type=pl.DeviceIdType.MESH)

    @pl.when(z > 0)
    def _():
        pl.semaphore_signal(barrier, inc=1, device_id={"tp": t - 2}, device_id_type=pl.DeviceIdType.MESH)

    @pl.when(z < 3)
    def _():
        pl.semaphore_signal(barrier, inc=1, device_id={"tp": t + 2}, device_id_type=pl.DeviceIdType.MESH)

    for n in range(SLOTS):
        fetch(jnp.int32(n))

    @pl.when(middle)
    def _():
        pl.semaphore_wait(barrier, 3)

    @pl.when(jnp.logical_not(middle))
    def _():
        pl.semaphore_wait(barrier, 2)

    @pl.loop(0, G)
    def _(q):
        send_own(line, across, q)

    @pl.loop(0, 4)
    def _(s):
        def step(r):
            held[s, r, :] = jnp.zeros((STRIP, D), F32)

        strips(step)

    mine = pltpu.make_async_copy(x, dyv.at[pl.ds(0, R), :], ios.at[0])
    mine.start()
    mine.wait()
    XP, XL = x_part.shape[1], x_late0.shape[1]
    mine = [
        pltpu.make_async_copy(dyv.at[pl.ds(0, R), pl.ds(0, XP)], x_part.at[rows(z, c), :], ios.at[0]),
        pltpu.make_async_copy(dyv.at[pl.ds(0, R), pl.ds(XP, XL)], x_late0, ios.at[1]),
        pltpu.make_async_copy(dyv.at[pl.ds(0, R), pl.ds(XP + XL, XL)], x_late1, ios.at[2]),
    ]
    for cp in mine:
        cp.start()

    e_in(jnp.int32(0)).start()

    @pl.loop(0, G)
    def _(q):
        @pl.loop(0, 4)
        def _(j):
            e_step(4 * q + j)

        pass_on(line, across, 1, q)

    for i in (4 * G - 2, 4 * G - 1):
        for cp in e_out(jnp.int32(i)):
            cp.wait()
    for cp in mine:
        cp.wait()

    mirror = z // 2
    u = z + mirror * (3 - 2 * z)

    def block(k):
        base = (1 - k // 3) * (k + 1) + (k // 3) * u - ((3 - k) // 3) * u
        return base + mirror * (3 - 2 * base)

    @pl.loop(0, 4)
    def _(k):
        s = block(k)

        for cp in slope_copies(s, 0):
            cp.start()

        @pl.when(k == 3)
        def _():
            pltpu.make_async_copy(dy, dyv.at[pl.ds(0, R), :], ios.at[0]).start()

        @pl.when(k < 3)
        def _():
            pltpu.make_async_copy(dy_all.at[rows(s, c), :], dyv.at[pl.ds(0, R), :], ios.at[0]).start()

        @pl.loop(0, G)
        def _(q):
            across(s, q).wait_recv()

        other = pltpu.make_async_copy(dy_all.at[rows(s, 1 - c), :], dyv.at[pl.ds(R, R), :], ios.at[1])
        other.start()
        pltpu.make_async_copy(dy, dyv.at[pl.ds(0, R), :], ios.at[0]).wait()

        keep = pltpu.make_async_copy(dyv.at[pl.ds(0, R), :], dy_all.at[rows(s, c), :], ios.at[0])

        @pl.when(k == 3)
        def _():
            keep.start()

        other.wait()

        @pl.loop(0, G)
        def _(m):
            n = 28 * k + 2 * m
            slot = ready(n)
            acc[...] = lax.dot_general(dyv[:, :F], ring[slot], NT, preferred_element_type=F32)
            fetch(n + SLOTS)
            slot = ready(n + 1)
            for cp in slope_copies(s, m):
                cp.wait()
            d_h = acc[...] + lax.dot_general(dyv[:, F:], ring[slot], NT, preferred_element_type=F32)
            dpre[:, tile(m)] = (d_h * slp[m % 2]).astype(BF16)
            fetch(n + 1 + SLOTS)

            @pl.when(m < G - 1)
            def _():
                for cp in slope_copies(s, m + 1):
                    cp.start()

            hooks(k, m)

            @pl.when(jnp.logical_and(m == 0, k > 0))
            def _():
                pair_add(k - 1, block(k - 1), G - 1)

            @pl.when(jnp.logical_and(k < 2, m % 2 == 1))
            def _():
                pass_on(line, across, k + 2, m // 2)

            @pl.when(m < XG)
            def _():
                @pl.when(jnp.logical_or(jnp.logical_and(k == 0, ends), jnp.logical_and(k == 1, middle)))
                def _():
                    send_own(x_line, x_across, m)

                @pl.when(jnp.logical_and(k == 2, middle))
                def _():
                    pass_on(x_line, x_across, 2, m)

                @pl.when(jnp.logical_and(k == 3, ends))
                def _():
                    pass_on(x_line, x_across, 1, m)
                    pass_on(x_line, x_across, 2, m)

        @pl.when(k == 3)
        def _():
            keep.wait()

        for cp in out_copies(s):
            cp.start()

        @pl.loop(0, G)
        def _(m):
            @pl.when(k > 0)
            def _():
                pair(k - 1, m).wait_send()

            for half in range(2):
                n = 28 * k + 14 + 2 * m + half
                slot = ready(n)
                term = lax.dot_general(dpre[...], ring[slot], NT, preferred_element_type=F32)
                held[s, :, tile(2 * m + half)] += term[:R]
                psend[:, tile(2 * m + half)] = term[R:].astype(BF16)
                fetch(n + SLOTS)
            @pl.when(m > 0)
            def _():
                pair_add(k, s, m - 1)

            pair(k, m).start()

            @pl.when(jnp.logical_and(k < 2, m % 2 == 0))
            def _():
                pass_on(line, across, k + 2, 3 + m // 2)

            @pl.when(m < XG)
            def _():
                @pl.when(jnp.logical_and(k == 1, middle))
                def _():
                    pass_on(x_line, x_across, 1, m)

                @pl.when(jnp.logical_and(k == 3, ends))
                def _():
                    pass_on(x_line, x_across, 3, m)

            hooks(k, G + m)


        late(k)

        @pl.when(jnp.logical_and(k == 1, middle))
        def _():
            pl.semaphore_signal(
                credit, inc=1, device_id={"tp": t - 2 + 4 * (z - 1)}, device_id_type=pl.DeviceIdType.MESH
            )

        @pl.when(k == 3)
        def _():
            pair_add(k, s, G - 1)

        for cp in out_copies(s):
            cp.wait()

    @pl.when(ends)
    def _():
        @pl.loop(0, GC)
        def _(g):
            arrive((3 - z) // 3, 3, g, False, False)

    @pl.loop(0, G)
    def _(g):
        pair(jnp.int32(3), g).wait_send()

        def step(r):
            psend[r, chunk(g)] = held[z, r, chunk(g)].astype(BF16)

        strips(step)

    out = pltpu.make_async_copy(psend, dx, ios.at[0])
    out.start()

    @pl.loop(0, GC)
    def _(q):
        @pl.when(middle)
        def _():
            chain(0, 3, q).wait_send()
            chain(1, 3, q).wait_send()

        @pl.when(jnp.logical_not(middle))
        def _():
            chain(z // 3, 3, q).wait_send()

    @pl.loop(0, G)
    def _(q):
        drain(line, across, q)

    @pl.loop(0, XG)
    def _(q):
        drain(x_line, x_across, q)
        for s in range(4):
            x_across(s, q).wait_recv()

    out.wait()


def gather_reduce(x, dy, pre, w_in, w_down):
    R, D = dy.shape
    rows, F = pre.shape
    T = F // G
    dma = pltpu.SemaphoreType.DMA
    any_spec = pl.BlockSpec(memory_space=pl.ANY)
    return pl.pallas_call(
        gather_reduce_kernel,
        name="gather_reduce",
        out_shape=(
            jax.ShapeDtypeStruct((rows, D), BF16),
            jax.ShapeDtypeStruct((rows, F), BF16),
            jax.ShapeDtypeStruct((rows, F), BF16),
            jax.ShapeDtypeStruct((R, D), BF16),
            jax.ShapeDtypeStruct((rows, XW * D // 7168), BF16),
            jax.ShapeDtypeStruct((rows, F), F32),
            jax.ShapeDtypeStruct((R, D - XW * D // 7168 - XL * D // 7168), BF16),
            jax.ShapeDtypeStruct((R, XL * D // 7168), BF16),
        ),
        in_specs=[any_spec] * 5,
        out_specs=[any_spec] * 8,
        scratch_shapes=[
            pltpu.VMEM((2 * R, D), BF16),
            pltpu.VMEM((SLOTS, T, F), BF16),
            pltpu.VMEM((2 * R, F), BF16),
            pltpu.VMEM((2, 2 * R, T), F32),
            pltpu.VMEM((4, R, D), F32),
            pltpu.VMEM((2, R, D), BF16),
            pltpu.VMEM((R, D), BF16),
            pltpu.VMEM((2, 2, R, D), BF16),
            pltpu.VMEM((2, R, D), BF16),
            pltpu.VMEM((2 * R, T), F32),
            dma((SLOTS, 2)),
            dma((4,)),
            dma((3, 2)),
            dma((2, 2)),
            dma((2, 3, G)),
            dma((4, G)),
            dma((4, G)),
            dma((4, G)),
            dma((2, 3, XG)),
            dma((4, XG)),
            dma((4, XG)),
            dma((4, XG)),
            dma((G,)),
            dma((2, G)),
            dma((2, GC)),
            dma((2, 2, GC)),
            pltpu.SemaphoreType.REGULAR,
        ],
        compiler_params=pltpu.CompilerParams(
            collective_id=0, has_side_effects=True, vmem_limit_bytes=VMEM
        ),
        cost_estimate=pl.CostEstimate(
            flops=4 * rows * D * F, bytes_accessed=16 * D * F, transcendentals=rows * F
        ),
    )(x, dy, pre, w_in, w_down)


def weight_grad_kernel(a, b, *rest, copied):
    o = rest[-1]
    if copied:
        rest[-2][...] = rest[-3][...]
    o[...] = lax.dot_general(a[...], b[...], TN, preferred_element_type=F32).astype(BF16)


def weight_grad(a, b, total, start, into, bm, bn, small=None):
    rows, A = a.shape
    B = b.shape[1]
    off = start // bm
    steps = A // bm
    args = [a, b]
    in_specs = [
        pl.BlockSpec((rows, bm), lambda j, i: (0, i)),
        pl.BlockSpec((rows, bn), lambda j, i: (0, j)),
    ]
    out_shape = [jax.ShapeDtypeStruct((total, B), BF16)]
    out_specs = [pl.BlockSpec((bm, bn), lambda j, i: (i + off, j))]
    aliases = {}
    if into is not None:
        aliases = {2: 0 if small is None else 1}
        args.append(into)
        in_specs.append(pl.BlockSpec(memory_space=pl.ANY))
    if small is not None:
        spec = pl.BlockSpec((small.shape[0] // steps, small.shape[1]), lambda j, i: (i, 0))
        args.append(small)
        in_specs.append(spec)
        out_shape.insert(0, jax.ShapeDtypeStruct(small.shape, BF16))
        out_specs.insert(0, spec)
    out = pl.pallas_call(
        functools.partial(weight_grad_kernel, copied=small is not None),
        name="weight_grad",
        grid=(B // bn, steps),
        out_shape=out_shape,
        in_specs=in_specs,
        out_specs=out_specs,
        input_output_aliases=aliases,
        compiler_params=pltpu.CompilerParams(
            dimension_semantics=("arbitrary", "arbitrary"), vmem_limit_bytes=VMEM
        ),
        cost_estimate=pl.CostEstimate(
            flops=2 * rows * A * B, bytes_accessed=2 * (rows * (A + B) + A * B), transcendentals=0
        ),
    )(*args)
    return out[0] if small is None else out


WITH_X, NOUT = True, 8


def solution(mesh):
    def body(x, dy, pre, w_in, w_down):
        dy_all, d_pre, hidden, dx, x_part, _, *late = gather_reduce(x, dy, pre, w_in, w_down)
        late = [lax.all_gather(piece, "tp", axis=0, tiled=True) for piece in late]
        D, F = w_in.shape
        dw_in = weight_grad(x_part, d_pre, D, 0, None, 1024, 1792)
        dw_down = weight_grad(hidden, dy_all, F, 0, None, 896, 1792)
        dw_in = weight_grad(late[0], d_pre, D, XW, dw_in, 512, 3584)
        dx, dw_in = weight_grad(late[1], d_pre, D, XW + XL, dw_in, 512, 3584, small=dx)
        return dx, dw_in, dw_down

    rows = P(("dp", "tp"), None)
    return jax.shard_map(
        body,
        mesh=mesh,
        in_specs=(rows, rows, P("dp", "tp"), P(None, "tp"), P("tp", None)),
        out_specs=(rows, P("dp", "tp"), P(("dp", "tp"), None)),
        check_vma=False,
    )
```

time: 524 us -> 451 us (0.86)
  waiting for transfers between devices: 57.4 us -> 2.88 us
  Pallas kernels: 445 us -> 434 us
  local copies, waits for them, and re-layouts: 7.8 us -> 0 us
    all_gather x3 -> x2, waiting for transfers between devices: 56.7 us -> 2.35 us  [body(): late = [lax.all_gather(piece, 'tp', axis=0, tiled=True) for piece in late]]
    pallas_call x1, Pallas kernels: 282 us -> 272 us  [gather_reduce(): pl.pallas_call(gather_reduce_kernel, name='gather_reduce', out_shape=(jax...]
  transfers between devices with their start and end apart: 3 -> 2, of which waited for: 2 -> 1; matrix products, arithmetic and copies ran while one was open for 0% -> 0% of each run, Pallas kernels for 25% -> 29%
where the time goes in v2:
time: 451 us
  Pallas kernels  434 us (96%)
  between operations  14 us (3%)
    pallas_call x1, Pallas kernels, gather_reduce(): pl.pallas_call(gather_reduce_kernel, name='gather_reduce', out_shape=(jax...  272 us
    pallas_call x4, Pallas kernels, weight_grad(): pl.pallas_call(functools.partial(weight_grad_kernel, copied=small is not...  162 us
  transfers between devices with their start and end apart: 2, of which 1 were waited for; matrix products, arithmetic and copies ran while one was open for 0% of the time, Pallas kernels for 29%

profile of v2, /device:TPU:0, one launch (start us, length us, event | category | flops | bytes accessed | tf_op | source)
XLA Modules:
  0.0 450.7 jit_solution(10662203310209999018)
XLA Ops:
  7.2 0.0 all-gather.5.cloned.1.call-start
  7.2 271.9 %gather_reduce.1 = (bf16[1280,7168]{1,0:T(8,128)(2,1)}, bf16[1280,3584]{1,0:T(8,128)(2,1)}, bf16[1280,3584]{1,0:T(8,128)(2,1)}, bf16[160,7168]{1,0:T(8,128)(2,1)...) custom-call(bf16[160,7168]{1,0:T(8,128)(2,1)} %x.1, ...), custom_call_target="tpu_custom_call" | custom-call | flops 131533373440 | bytes 411041792 | tf_op jit(solution)/shard_map/gather_reduce/pallas_call | solution.py:568
  279.1 0.0 all-gather.5.cloned.1.call-update
  279.1 0.2 all-gather.3.cloned.1.call-start
  279.3 0.5 all-gather.3.cloned.1.call-update
  279.8 25.0 %weight_grad.4.rest_0_ = bf16[7168,3584]{1,0:T(8,128)(2,1)} custom-call(bf16[1280,2048]{1,0:T(8,128)(2,1)} %get-tuple-element.15.a, bf16[1280,3584]{1,0:T(8,128)(2,1)} %get-tuple-element.13.b), custom_call_target="tpu_custom_call" | custom-call | flops 18790481920 | bytes 29097984 | tf_op jit(solution)/shard_map/weight_grad/pallas_call | solution.py:651
  304.9 75.0 %weight_grad.7 = bf16[3584,7168]{1,0:T(8,128)(2,1)} custom-call(bf16[1280,3584]{1,0:T(8,128)(2,1)} %get-tuple-element.19.a, bf16[1280,7168]{1,0:T(8,128)(2,1)} %get-tuple-element.20.b), custom_call_target="tpu_custom_call" | custom-call | flops 65766686720 | bytes 78905344 | tf_op jit(solution)/shard_map/weight_grad/pallas_call | solution.py:651
  379.9 0.0 all-gather.5.cloned.1.call-done.a
  379.9 30.8 %weight_grad.5.rest_0_ = bf16[7168,3584]{1,0:T(8,128)(2,1)} custom-call(bf16[1280,2560]{1,0:T(8,128)(2,1)} %all-gather.5.cloned.1.call-done.a, bf16[1280,3584]{1,0:T(8,128)(2,1)} %get-tuple-element.13.b, bf16[7168,3584]{1,0:T(8,128)(2,1)} %weight_grad.4.rest_0_), custom_call_target="tpu_custom_call", output_to_operand_aliasing={{}: (2, {})} | custom-call | flops 23488102400 | bytes 34078720 | tf_op jit(solution)/shard_map/weight_grad/pallas_call | solution.py:651
  410.6 2.3 all-gather.3.cloned.1.call-done.a
  413.0 30.9 %weight_grad.6 = (bf16[160,7168]{1,0:T(8,128)(2,1)}, bf16[7168,3584]{1,0:T(8,128)(2,1)}) custom-call(bf16[1280,2560]{1,0:T(8,128)(2,1)} %all-gather.3.cloned.1.call-done.a, bf16[1280,3584]{1,0:T(8,128)(2,1)} %get-tuple-element.13.b, bf16[7168,3584]{1,0:T(8,128)(2,1)} %weight_grad.5.rest_0_, ...), custom_call_target="tpu_custom_call", output_to_operand_aliasing={{1}: (2, {})} | custom-call | flops 23488102400 | bytes 34078720 | tf_op jit(solution)/shard_map/weight_grad/pallas_call | solution.py:651
Async XLA Ops:
  7.2 372.7 %all-gather.5.cloned.1.call-start = ((), (), s32[]{:S(2)}) async-start(), calls=%async_computation.1 | async-start | bytes 7372800 | tf_op jit(solution)/shard_map/all_gather | solution.py:675
  279.1 133.9 %all-gather.3.cloned.1.call-start = ((), (), s32[]{:S(2)}) async-start(), calls=%async_computation | async-start | bytes 7372800 | tf_op jit(solution)/shard_map/all_gather | solution.py:675
Sparse Core Ops, SparseCore 0:
  279.2 66.5 all-gather.4
  347.4 65.4 all-gather.2

commit v3 on v2

v3 whole, which is shorter than its diff:
```python
import functools

import jax
import jax.numpy as jnp
from jax import lax
from jax.experimental import pallas as pl
from jax.experimental.pallas import tpu as pltpu
from jax.sharding import PartitionSpec as P

F32, BF16 = jnp.float32, jnp.bfloat16
NT = (((1,), (1,)), ((), ()))
TN = (((0,), (0,)), ((), ()))
G = 7
STRIP = 16
SLOTS = 4
VMEM = 67043328
XG = 9
GC = 14
BI, BJ = 4, 4
XG = 9
GC = 14
XL = 2560
NB = 5
XW = 4608
XL = 2048
C0 = 0.7978845608028654
C1 = 0.044715


def gather_reduce_kernel(
    x, dy, pre, w_in, w_down, dy_all, d_pre, hidden, dx, x_part, x_late0, x_late1, down,
    held, precv, psend, crecv, cs,
    ws, ios, hos, prs, ls, lr, ps, pr, xls, xlr, xps, xpr, pss, psr, css, csr, fas, fbs, fos, credit,
):
    R, D = dy.shape
    F = pre.shape[1]
    CH, T = D // G, F // G
    XC = x_part.shape[1] // XG
    t = lax.axis_index("tp")
    z, c = t // 2, t % 2
    partner = t + 1 - 2 * c

    def rows(s, core):
        return pl.ds(pl.multiple_of((2 * s + core) * R, R), R)

    def chunk(q):
        return pl.ds(pl.multiple_of(q * CH, CH), CH)

    def slab(q):
        return pl.ds(pl.multiple_of(q * (D // GC), D // GC), D // GC)

    def tile(j):
        return pl.ds(pl.multiple_of(j * T, T), T)

    def remote(src, dst, send, recv, to):
        return pltpu.make_async_remote_copy(
            src_ref=src, dst_ref=dst, send_sem=send, recv_sem=recv,
            device_id={"tp": to}, device_id_type=pl.DeviceIdType.MESH,
        )

    def line(way, hop, s, q, own=False):
        here = dy_all.at[rows(s, c), chunk(q)]
        src = dy.at[:, chunk(q)] if own else here
        return remote(src, here, ls.at[way, hop, q], lr.at[s, q], t + 2 - 4 * way)

    def across(s, q, own=False):
        here = dy_all.at[rows(s, c), chunk(q)]
        src = dy.at[:, chunk(q)] if own else here
        return remote(src, here, ps.at[s, q], pr.at[s, q], partner)

    def xcols(q):
        return pl.ds(pl.multiple_of(q * XC, XC), XC)

    def x_line(way, hop, s, q, own=False):
        here = x_part.at[rows(s, c), xcols(q)]
        src = x.at[:, xcols(q)] if own else here
        return remote(src, here, xls.at[way, hop, q], xlr.at[s, q], t + 2 - 4 * way)

    def x_across(s, q, own=False):
        here = x_part.at[rows(s, c), xcols(q)]
        src = x.at[:, xcols(q)] if own else here
        return remote(src, here, xps.at[s, q], xpr.at[s, q], partner)

    def send_own(along, over, q):
        over(z, q, own=True).start()

        @pl.when(z < 3)
        def _():
            along(0, 0, z, q, own=True).start()

        @pl.when(z > 0)
        def _():
            along(1, 0, z, q, own=True).start()

    def pass_on(along, over, hop, q):
        @pl.when(z >= hop)
        def _():
            along(0, hop, z - hop, q).wait_recv()

            @pl.when(z < 3)
            def _():
                along(0, hop, z - hop, q).start()

            over(z - hop, q).start()

        @pl.when(z + hop <= 3)
        def _():
            along(1, hop, z + hop, q).wait_recv()

            @pl.when(z > 0)
            def _():
                along(1, hop, z + hop, q).start()

            over(z + hop, q).start()

    def drain(along, over, q):
        for hop in range(3):

            @pl.when(jnp.logical_and(z >= hop, z < 3))
            def _():
                along(0, hop, z, q).wait_send()

            @pl.when(jnp.logical_and(z + hop <= 3, z > 0))
            def _():
                along(1, hop, z, q).wait_send()

        for s in range(4):
            over(s, q).wait_send()

    def pair(k, g):
        return remote(
            psend.at[:, chunk(g)], precv.at[:, chunk(g)], pss.at[g], psr.at[g], partner
        )

    def chain(way, a, g):
        return remote(
            cs.at[way, :, slab(g)], crecv.at[way, (a - 1) % 2, :, slab(g)],
            css.at[way, g], csr.at[way, (a - 1) % 2, g], t + 2 - 4 * way,
        )

    def strips(step):
        @pl.loop(0, R // STRIP)
        def _(i):
            step(pl.ds(pl.multiple_of(i * STRIP, STRIP), STRIP))

    def pair_add(k, s, g):
        pair(k, g).wait_recv()
        source = jnp.logical_and(z % 3 == 0, k > 0)
        way = z // 3

        @pl.when(source)
        def _():
            @pl.when(jnp.logical_and(k == 3, g == 0))
            def _():
                pl.semaphore_wait(credit, 1)

            @pl.loop(0, GC // G)
            def _(j):
                piece = g * (GC // G) + j

                @pl.when(k >= 2)
                def _():
                    chain(way, k, piece).wait_send()

                def step(r):
                    total = held[s, r, slab(piece)] + precv[r, slab(piece)].astype(F32)
                    cs[way, r, slab(piece)] = total.astype(BF16)

                strips(step)
                chain(way, k, piece).start()

        @pl.when(jnp.logical_not(source))
        def _():
            def step(r):
                held[s, r, chunk(g)] += precv[r, chunk(g)].astype(F32)

            strips(step)

    def arrive(way, a, g, forward, sent_before):
        d = a + way * (3 - 2 * a)
        chain(way, a, g).wait_recv()
        old = (a - 1) % 2

        @pl.when(forward)
        def _():
            @pl.when(sent_before)
            def _():
                chain(way, a, g).wait_send()

            def step(r):
                total = held[d, r, slab(g)] + crecv[way, old, r, slab(g)].astype(F32)
                cs[way, r, slab(g)] = total.astype(BF16)

            strips(step)
            chain(way, a, g).start()

        @pl.when(jnp.logical_not(forward))
        def _():
            def step(r):
                held[d, r, slab(g)] += crecv[way, old, r, slab(g)].astype(F32)

            strips(step)

    middle = jnp.logical_and(z >= 1, z <= 2)
    ends = z % 3 == 0

    def hooks(k, v):
        @pl.when(jnp.logical_and(k < 3, v % 2 == 1))
        def _():
            pass_on(line, across, k + 1, v // 2)

        def x_pair(v, step):
            for j in range(2):

                @pl.when(jnp.logical_and(v >= 0, 2 * v + j < XG))
                def _():
                    step(2 * v + j)

        @pl.when(jnp.logical_or(jnp.logical_and(k == 1, ends), jnp.logical_and(k == 2, middle)))
        def _():
            x_pair(v, lambda q: send_own(x_line, x_across, q))

        @pl.when(jnp.logical_and(k == 2, middle))
        def _():
            x_pair(v - G, lambda q: pass_on(x_line, x_across, 1, q))

        @pl.when(jnp.logical_and(k == 3, middle))
        def _():
            x_pair(v, lambda q: pass_on(x_line, x_across, 2, q))

        @pl.when(jnp.logical_and(k >= 2, middle))
        def _():
            @pl.when(v == 0)
            def _():
                @pl.loop(0, 3)
                def _(g):
                    arrive(z - 1, k - 1, g, k == 3, False)

            @pl.when(v <= 10)
            def _():
                arrive(z - 1, k - 1, v + 3, k == 3, False)

    def tail_hooks(f):
        def sums(j, way, a, forward, sent_before):
            @pl.loop(0, 2)
            def _(i):
                arrive(way, a, 2 * j + i, forward, sent_before)

        @pl.when(middle)
        def _():
            @pl.when(f < 7)
            def _():
                sums(f, z - 1, 3, True, True)

            @pl.when(jnp.logical_and(jnp.logical_and(f >= 3, f <= 12), f % 3 < 2))
            def _():
                sums(2 * (f // 3 - 1) + f % 3, 2 - z, 3, True, False)

            @pl.when(jnp.logical_and(jnp.logical_and(f >= 5, f <= 11), f % 3 == 2))
            def _():
                @pl.loop(0, 5)
                def _(i):
                    g = 5 * (f // 3 - 1) + i

                    @pl.when(g < GC)
                    def _():
                        arrive(2 - z, 2, g, False, False)

        @pl.when(ends)
        def _():
            def x_four(f, hop):
                for j in range(4):

                    @pl.when(4 * f + j < XG)
                    def _():
                        pass_on(x_line, x_across, hop, 4 * f + j)

            @pl.when(f < 3)
            def _():
                x_four(f, 1)

            @pl.when(jnp.logical_and(f >= 3, f < 6))
            def _():
                x_four(f - 3, 2)

            @pl.when(jnp.logical_and(f >= 9, f < 12))
            def _():
                x_four(f - 9, 3)

            @pl.when(jnp.logical_and(jnp.logical_and(f >= 8, f <= 15), f % 3 != 1))
            def _():
                sums(2 * ((f - 8) // 3) + (f - 8) % 3, (3 - z) // 3, 3, False, False)

    barrier = pltpu.get_barrier_semaphore()
    pl.semaphore_signal(barrier, inc=1, device_id={"tp": partner}, device_id_type=pl.DeviceIdType.MESH)

    @pl.when(z > 0)
    def _():
        pl.semaphore_signal(barrier, inc=1, device_id={"tp": t - 2}, device_id_type=pl.DeviceIdType.MESH)

    @pl.when(z < 3)
    def _():
        pl.semaphore_signal(barrier, inc=1, device_id={"tp": t + 2}, device_id_type=pl.DeviceIdType.MESH)


    @pl.when(middle)
    def _():
        pl.semaphore_wait(barrier, 3)

    @pl.when(jnp.logical_not(middle))
    def _():
        pl.semaphore_wait(barrier, 2)

    @pl.loop(0, G)
    def _(q):
        send_own(line, across, q)

    stage = pltpu.make_async_copy(x, psend, fos.at[0])
    stage.start()
    XP, XA = x_part.shape[1], x_late0.shape[1]
    staged = [
        pltpu.make_async_copy(psend.at[:, pl.ds(0, XP)], x_part.at[rows(z, c), :], fos.at[0]),
        pltpu.make_async_copy(psend.at[:, pl.ds(XP, XA)], x_late0, fos.at[1]),
        pltpu.make_async_copy(psend.at[:, pl.ds(XP + XA, D - XP - XA)], x_late1, fas.at[0]),
    ]

    mirror = z // 2
    u = z + mirror * (3 - 2 * z)

    def block(k):
        base = (k // 2) * k + (1 - k // 2) * ((k + u) % 2)
        return base + mirror * (3 - 2 * base)

    def passes(dyv, ring, dpre, hid, preb, acc):
        H = T // 2

        def load(src, lo, n, slot, part):
            return pltpu.make_async_copy(
                src, ring.at[slot, pl.ds(part * H, H), :], ws.at[slot, part]
            )

        def fetch(n):
            i, slot = n % 28, n % SLOTS

            @pl.when(n < 112)
            def _():
                for part in range(2):

                    @pl.when(i < 14)
                    def _():
                        src = w_down.at[
                            pl.ds(pl.multiple_of((i // 2) * T + part * H, H), H),
                            pl.ds(pl.multiple_of((i % 2) * F, F), F),
                        ]
                        load(src, 0, n, slot, part).start()

                    @pl.when(i >= 14)
                    def _():
                        src = w_in.at[pl.ds(pl.multiple_of((i - 14) * T + part * H, H), H), :]
                        load(src, 0, n, slot, part).start()

        def ready(n):
            slot = n % SLOTS
            for part in range(2):
                load(w_in.at[pl.ds(0, H), :], 0, n, slot, part).wait()
            return slot

        def pre_copies(s, m):
            return [
                pltpu.make_async_copy(
                    pre.at[rows(s, core), tile(m)], preb.at[m % 2, pl.ds(i * R, R), :], prs.at[m % 2, i]
                )
                for i, core in enumerate((c, 1 - c))
            ]

        def hid_copies(s, m):
            return [
                pltpu.make_async_copy(
                    hid.at[m % 2, pl.ds(i * R, R), :], hidden.at[rows(s, core), tile(m)], hos.at[m % 2, i]
                )
                for i, core in enumerate((c, 1 - c))
            ]

        def out_copies(s):
            return [
                pltpu.make_async_copy(dpre.at[pl.ds(i * R, R), :], d_pre.at[rows(s, core), :], ios.at[2 + i])
                for i, core in enumerate((c, 1 - c))
            ]

        for n in range(SLOTS):
            fetch(jnp.int32(n))

        @pl.loop(0, 4)
        def _(k):
            s = block(k)

            for cp in pre_copies(s, 0):
                cp.start()

            @pl.when(k == 0)
            def _():
                pltpu.make_async_copy(dy, dyv.at[pl.ds(0, R), :], ios.at[0]).start()

            @pl.when(k > 0)
            def _():
                pltpu.make_async_copy(dy_all.at[rows(s, c), :], dyv.at[pl.ds(0, R), :], ios.at[0]).start()

            @pl.loop(0, G)
            def _(q):
                across(s, q).wait_recv()

            other = pltpu.make_async_copy(dy_all.at[rows(s, 1 - c), :], dyv.at[pl.ds(R, R), :], ios.at[1])
            other.start()
            pltpu.make_async_copy(dy, dyv.at[pl.ds(0, R), :], ios.at[0]).wait()

            keep = pltpu.make_async_copy(dyv.at[pl.ds(0, R), :], dy_all.at[rows(s, c), :], ios.at[0])

            @pl.when(k == 0)
            def _():
                keep.start()
                stage.wait()
                for cp in staged:
                    cp.start()

            other.wait()

            @pl.loop(0, G)
            def _(m):
                n = 28 * k + 2 * m

                @pl.when(m < G - 1)
                def _():
                    for cp in pre_copies(s, m + 1):
                        cp.start()

                slot = ready(n)
                acc[...] = lax.dot_general(dyv[:, :F], ring[slot], NT, preferred_element_type=F32)
                fetch(n + SLOTS)
                slot = ready(n + 1)
                acc[...] += lax.dot_general(dyv[:, F:], ring[slot], NT, preferred_element_type=F32)
                fetch(n + 1 + SLOTS)
                for cp in pre_copies(s, m):
                    cp.wait()

                @pl.when(m >= 2)
                def _():
                    for cp in hid_copies(s, m - 2):
                        cp.wait()

                @pl.loop(0, 2 * R // STRIP)
                def _(i):
                    strip = pl.ds(pl.multiple_of(i * STRIP, STRIP), STRIP)
                    v = preb[m % 2, strip, :].astype(F32)
                    sq = v * v
                    th = jnp.tanh(v * (C0 + (C0 * C1) * sq))
                    cdf = 0.5 + 0.5 * th
                    slope = cdf + (v * (1.0 - th * th)) * (0.5 * C0 + (1.5 * C0 * C1) * sq)
                    dpre[strip, tile(m)] = (acc[strip, :] * slope).astype(BF16)
                    hid[m % 2, strip, :] = (v * cdf).astype(BF16)

                for cp in hid_copies(s, m):
                    cp.start()

                hooks(k, m)

                @pl.when(jnp.logical_and(m == 0, k > 0))
                def _():
                    pair_add(k - 1, block(k - 1), G - 1)

            @pl.when(k == 0)
            def _():
                keep.wait()
                for cp in staged:
                    cp.wait()

            for m in (G - 2, G - 1):
                for cp in hid_copies(s, m):
                    cp.wait()

            for cp in out_copies(s):
                cp.start()

            @pl.loop(0, G)
            def _(m):
                @pl.when(k > 0)
                def _():
                    pair(k - 1, m).wait_send()

                for half in range(2):
                    n = 28 * k + 14 + 2 * m + half
                    slot = ready(n)
                    term = lax.dot_general(dpre[...], ring[slot], NT, preferred_element_type=F32)
                    held[s, :, tile(2 * m + half)] = term[:R]
                    psend[:, tile(2 * m + half)] = term[R:].astype(BF16)
                    fetch(n + SLOTS)
                @pl.when(m > 0)
                def _():
                    pair_add(k, s, m - 1)

                pair(k, m).start()

                hooks(k, G + m)


            @pl.when(jnp.logical_and(k == 2, middle))
            def _():
                pl.semaphore_signal(
                    credit, inc=1, device_id={"tp": t - 2 + 4 * (z - 1)}, device_id_type=pl.DeviceIdType.MESH
                )

            @pl.when(k == 3)
            def _():
                pair_add(k, s, G - 1)

            for cp in out_copies(s):
                cp.wait()

    pl.run_scoped(
        passes,
        pltpu.VMEM((2 * R, D), BF16),
        pltpu.VMEM((SLOTS, T, F), BF16),
        pltpu.VMEM((2 * R, F), BF16),
        pltpu.VMEM((2, 2 * R, T), BF16),
        pltpu.VMEM((2, 2 * R, T), BF16),
        pltpu.VMEM((2 * R, T), F32),
    )

    TI, TJ = F // BI, D // BJ

    def fill(fa, fb, fo):
        def strip(i, size):
            return pl.ds(pl.multiple_of(i * size, size), size)

        def a_copy(i):
            return pltpu.make_async_copy(hidden.at[:, strip(i, TI)], fa.at[i % 2], fas.at[i % 2])

        def b_copy(f):
            return pltpu.make_async_copy(dy_all.at[:, strip(f % BJ, TJ)], fb.at[f % 2], fbs.at[f % 2])

        def o_copy(f):
            return pltpu.make_async_copy(
                fo.at[f % 2], down.at[strip(f // BJ, TI), strip(f % BJ, TJ)], fos.at[f % 2]
            )

        a_copy(jnp.int32(0)).start()
        b_copy(jnp.int32(0)).start()

        @pl.loop(0, BI * BJ)
        def _(f):
            i = f // BJ

            @pl.when(f + 1 < BI * BJ)
            def _():
                b_copy(f + 1).start()

            @pl.when(f % BJ == 0)
            def _():
                @pl.when(i + 1 < BI)
                def _():
                    a_copy(i + 1).start()

                a_copy(i).wait()

            b_copy(f).wait()

            @pl.when(f >= 2)
            def _():
                o_copy(f - 2).wait()

            fo[f % 2] = lax.dot_general(
                fa[i % 2], fb[f % 2], TN, preferred_element_type=F32
            ).astype(BF16)
            o_copy(f).start()
            tail_hooks(f)

        for f in (BI * BJ - 2, BI * BJ - 1):
            o_copy(jnp.int32(f)).wait()

    pl.run_scoped(
        fill,
        pltpu.VMEM((2, 8 * R, TI), BF16),
        pltpu.VMEM((2, 8 * R, TJ), BF16),
        pltpu.VMEM((2, TI, TJ), BF16),
    )

    @pl.when(ends)
    def _():
        @pl.loop(GC - 2, GC)
        def _(g):
            arrive((3 - z) // 3, 3, g, False, False)

    @pl.loop(0, G)
    def _(g):
        pair(jnp.int32(3), g).wait_send()

        def step(r):
            psend[r, chunk(g)] = held[z, r, chunk(g)].astype(BF16)

        strips(step)

    out = pltpu.make_async_copy(psend, dx, ios.at[0])
    out.start()

    @pl.loop(0, GC)
    def _(q):
        @pl.when(middle)
        def _():
            chain(0, 3, q).wait_send()
            chain(1, 3, q).wait_send()

        @pl.when(jnp.logical_not(middle))
        def _():
            chain(z // 3, 3, q).wait_send()

    @pl.loop(0, G)
    def _(q):
        drain(line, across, q)

    @pl.loop(0, XG)
    def _(q):
        drain(x_line, x_across, q)
        for s in range(4):
            x_across(s, q).wait_recv()

    out.wait()


def gather_reduce(x, dy, pre, w_in, w_down):
    R, D = dy.shape
    rows, F = pre.shape
    T = F // G
    dma = pltpu.SemaphoreType.DMA
    any_spec = pl.BlockSpec(memory_space=pl.ANY)
    return pl.pallas_call(
        gather_reduce_kernel,
        name="gather_reduce",
        out_shape=(
            jax.ShapeDtypeStruct((rows, D), BF16),
            jax.ShapeDtypeStruct((rows, F), BF16),
            jax.ShapeDtypeStruct((rows, F), BF16),
            jax.ShapeDtypeStruct((R, D), BF16),
            jax.ShapeDtypeStruct((rows, XW * D // 7168), BF16),
            jax.ShapeDtypeStruct((R, XL * D // 7168), BF16),
            jax.ShapeDtypeStruct((R, D - (XW + XL) * D // 7168), BF16),
            jax.ShapeDtypeStruct((F, D), BF16),
        ),
        in_specs=[any_spec] * 5,
        out_specs=[any_spec] * 8,
        scratch_shapes=[
            pltpu.VMEM((4, R, D), F32),
            pltpu.VMEM((R, D), BF16),
            pltpu.VMEM((R, D), BF16),
            pltpu.VMEM((2, 2, R, D), BF16),
            pltpu.VMEM((2, R, D), BF16),
            dma((SLOTS, 2)),
            dma((4,)),
            dma((2, 2)),
            dma((2, 2)),
            dma((2, 3, G)),
            dma((4, G)),
            dma((4, G)),
            dma((4, G)),
            dma((2, 3, XG)),
            dma((4, XG)),
            dma((4, XG)),
            dma((4, XG)),
            dma((G,)),
            dma((G,)),
            dma((2, GC)),
            dma((2, 2, GC)),
            dma((2,)),
            dma((2,)),
            dma((2,)),
            pltpu.SemaphoreType.REGULAR,
        ],
        compiler_params=pltpu.CompilerParams(
            collective_id=0, has_side_effects=True, vmem_limit_bytes=VMEM
        ),
        cost_estimate=pl.CostEstimate(
            flops=4 * rows * D * F, bytes_accessed=16 * D * F, transcendentals=rows * F
        ),
    )(x, dy, pre, w_in, w_down)


def weight_grad_kernel(a, b, source, *rest, first, size, steps, small, aliased):
    if small:
        tiny, rest = rest[0], rest[1:]
    rest = rest[aliased:]
    o, target, rest = rest[0], rest[1], rest[2:]
    if small:
        tiny_out, *rest, tiny_buf, tiny_sem = rest
        tiny_in = pltpu.make_async_copy(tiny, tiny_buf, tiny_sem)
        tiny_out = pltpu.make_async_copy(tiny_buf, tiny_out, tiny_sem)
    buf, take, give = rest
    n = pl.program_id(0) * pl.num_programs(1) + pl.program_id(1)

    def part(i):
        return pl.ds(pl.multiple_of(first + i * size, size), size)

    def into(i):
        return pltpu.make_async_copy(source.at[part(i)], buf.at[i % 3], take.at[i % 3])

    def out(i):
        return pltpu.make_async_copy(buf.at[i % 3], target.at[part(i)], give.at[i % 3])

    @pl.when(n == 0)
    def _():
        into(n).start()
        if small:
            tiny_in.start()

    if small:

        @pl.when(n == 1)
        def _():
            tiny_in.wait()
            tiny_out.start()

    @pl.when(n >= 2)
    def _():
        out(n - 2).wait()

    @pl.when(n + 1 < steps)
    def _():
        into(n + 1).start()

    into(n).wait()
    out(n).start()
    o[...] = lax.dot_general(a[...], b[...], TN, preferred_element_type=F32).astype(BF16)

    @pl.when(n == steps - 1)
    def _():
        if steps > 1:
            out(n - 1).wait()
        out(n).wait()
        if small:
            tiny_out.wait()


def weight_grad(a, b, total, into, start, bm, bn, source, target, first, last, small=None):
    rows, A = a.shape
    B = b.shape[1]
    off, tall, wide = start // bm, A // bm, B // bn
    steps = tall * wide
    size = (last - first) // steps
    any_spec = pl.BlockSpec(memory_space=pl.ANY)
    args = [a, b, source]
    in_specs = [
        pl.BlockSpec((rows, bm), lambda j, i: (0, i)),
        pl.BlockSpec((rows, bn), lambda j, i: (0, j)),
        any_spec,
    ]
    out_shape = [jax.ShapeDtypeStruct((total, B), BF16), jax.ShapeDtypeStruct(source.shape, BF16)]
    out_specs = [pl.BlockSpec((bm, bn), lambda j, i: (i + off, j)), any_spec]
    if small is not None:
        args.append(small)
        in_specs.append(any_spec)
        out_shape.append(jax.ShapeDtypeStruct(small.shape, BF16))
        out_specs.append(any_spec)
    aliases = {}
    for n, array in enumerate((into, target)):
        if array is not None:
            aliases[len(args)] = n
            args.append(array)
            in_specs.append(any_spec)
    return pl.pallas_call(
        functools.partial(
            weight_grad_kernel,
            first=first, size=size, steps=steps, small=small is not None, aliased=len(aliases),
        ),
        name="weight_grad",
        grid=(wide, tall),
        out_shape=out_shape,
        in_specs=in_specs,
        out_specs=out_specs,
        scratch_shapes=[
            pltpu.VMEM((3, size, source.shape[1]), BF16),
            pltpu.SemaphoreType.DMA((3,)),
            pltpu.SemaphoreType.DMA((3,)),
        ]
        + ([] if small is None else [pltpu.VMEM(small.shape, BF16), pltpu.SemaphoreType.DMA]),
        input_output_aliases=aliases,
        compiler_params=pltpu.CompilerParams(
            dimension_semantics=("arbitrary", "arbitrary"), vmem_limit_bytes=VMEM
        ),
        cost_estimate=pl.CostEstimate(
            flops=2 * rows * A * B, bytes_accessed=2 * (rows * (A + B) + A * B), transcendentals=0
        ),
    )(*args)


WITH_X, NOUT = True, 8


def solution(mesh):
    def body(x, dy, pre, w_in, w_down):
        _, d_pre, _, dx, x_part, *late, down = gather_reduce(x, dy, pre, w_in, w_down)
        late = [lax.all_gather(piece, "tp", axis=0, tiled=True) for piece in late]
        D, F = w_in.shape
        dw_in, dw_down, dx = weight_grad(
            x_part, d_pre, D, None, 0, 512, 3584, down, None, 0, 2304, small=dx
        )
        dw_in, dw_down = weight_grad(
            late[0], d_pre, D, dw_in, XW, 512, 3584, down, dw_down, 2304, 3328
        )
        dw_in, dw_down = weight_grad(
            late[1], d_pre, D, dw_in, XW + XL, 512, 896, down, dw_down, 3328, F
        )
        return dx, dw_in, dw_down

    rows = P(("dp", "tp"), None)
    return jax.shard_map(
        body,
        mesh=mesh,
        in_specs=(rows, rows, P("dp", "tp"), P(None, "tp"), P("tp", None)),
        out_specs=(rows, P("dp", "tp"), P(("dp", "tp"), None)),
        check_vma=False,
    )
```

time: 451 us -> 413 us (0.916)
  Pallas kernels: 434 us -> 397 us
    pallas_call x4 -> x3, Pallas kernels: 162 us -> 94.7 us  [weight_grad(): pl.pallas_call(functools.partial(weight_grad_kernel, first=first, size=si...]
    pallas_call x1, Pallas kernels: 272 us -> 303 us  [gather_reduce(): pl.pallas_call(gather_reduce_kernel, name='gather_reduce', out_shape=(jax...]
  transfers between devices with their start and end apart: 2 -> 2, of which waited for: 1 -> 1; matrix products, arithmetic and copies ran while one was open for 0% -> 0% of each run, Pallas kernels for 29% -> 20%
where the time goes in v3:
time: 413 us
  Pallas kernels  397 us (96%)
  between operations  14.1 us (3%)
    pallas_call x1, Pallas kernels, gather_reduce(): pl.pallas_call(gather_reduce_kernel, name='gather_reduce', out_shape=(jax...  303 us
    pallas_call x3, Pallas kernels, weight_grad(): pl.pallas_call(functools.partial(weight_grad_kernel, first=first, size=si...  94.7 us
  transfers between devices with their start and end apart: 2, of which 1 were waited for; matrix products, arithmetic and copies ran while one was open for 0% of the time, Pallas kernels for 20%

profile of v3, /device:TPU:0, one launch (start us, length us, event | category | flops | bytes accessed | tf_op | source)
XLA Modules:
  0.0 412.8 jit_solution(11762374403573103747)
XLA Ops:
  7.2 0.0 all-gather.5.cloned.1.call-start
  7.2 302.7 %gather_reduce.1 = (bf16[1280,7168]{1,0:T(8,128)(2,1)}, bf16[1280,3584]{1,0:T(8,128)(2,1)}, bf16[1280,3584]{1,0:T(8,128)(2,1)}, bf16[160,7168]{1,0:T(8,128)(2,1)...) custom-call(bf16[160,7168]{1,0:T(8,128)(2,1)} %x.1, ...), custom_call_target="tpu_custom_call" | custom-call | flops 131533373440 | bytes 411041792 | tf_op jit(solution)/shard_map/gather_reduce/pallas_call | solution.py:634
  309.9 0.0 all-gather.5.cloned.1.call-update
  309.9 0.2 all-gather.3.cloned.1.call-start
  310.2 0.5 all-gather.3.cloned.1.call-update
  310.7 54.9 %weight_grad.3 = (bf16[7168,3584]{1,0:T(8,128)(2,1)}, bf16[3584,7168]{1,0:T(8,128)(2,1)}, bf16[160,7168]{1,0:T(8,128)(2,1)}) custom-call(bf16[1280,4608]{1,0:T(8,128)(2,1)} %get-tuple-element.16.a, bf16[1280,3584]{1,0:T(8,128)(2,1)} %get-tuple-element.17.b, bf16[3584,7168]{1,0:T(8,128)(2,1)} %get-tuple-element.18.source, ...), custom_call_target="tpu_custom_call" | custom-call | flops 42278584320 | bytes 54001664 | tf_op jit(solution)/shard_map/weight_grad/pallas_call | solution.py:766
  365.6 0.6 all-gather.5.cloned.1.call-done.a
  366.2 28.0 %weight_grad.4 = (bf16[7168,3584]{1,0:T(8,128)(2,1)}, bf16[3584,7168]{1,0:T(8,128)(2,1)}) custom-call(bf16[1280,2048]{1,0:T(8,128)(2,1)} %all-gather.5.cloned.1.call-done.a, bf16[1280,3584]{1,0:T(8,128)(2,1)} %get-tuple-element.17.b, bf16[3584,7168]{1,0:T(8,128)(2,1)} %get-tuple-element.18.source, ...), custom_call_target="tpu_custom_call", output_to_operand_aliasing={{0}: (3, {}), {1}: (4, {})} | custom-call | flops 18790481920 | bytes 29097984 | tf_op jit(solution)/shard_map/weight_grad/pallas_call | solution.py:766
  394.2 0.0 all-gather.3.cloned.1.call-done.a
  394.2 11.7 %weight_grad.5 = (bf16[7168,3584]{1,0:T(8,128)(2,1)}, bf16[3584,7168]{1,0:T(8,128)(2,1)}) custom-call(bf16[1280,512]{1,0:T(8,128)(2,1)} %all-gather.3.cloned.1.call-done.a, bf16[1280,3584]{1,0:T(8,128)(2,1)} %get-tuple-element.17.b, bf16[3584,7168]{1,0:T(8,128)(2,1)} %get-tuple-element.18.source, ...), custom_call_target="tpu_custom_call", output_to_operand_aliasing={{0}: (3, {}), {1}: (4, {})} | custom-call | flops 4697620480 | bytes 14155776 | tf_op jit(solution)/shard_map/weight_grad/pallas_call | solution.py:766
Async XLA Ops:
  7.2 359.0 %all-gather.5.cloned.1.call-start = ((), (), s32[]{:S(2)}) async-start(), calls=%async_computation.1 | async-start | bytes 5898240 | tf_op jit(solution)/shard_map/all_gather | solution.py:798
  309.9 84.3 %all-gather.3.cloned.1.call-start = ((), (), s32[]{:S(2)}) async-start(), calls=%async_computation | async-start | bytes 1474560 | tf_op jit(solution)/shard_map/all_gather | solution.py:798
Sparse Core Ops, SparseCore 0:
  310.1 56.0 all-gather.4
  367.8 22.1 all-gather.2

commit v4 on v3

--- a/solution.py
+++ b/solution.py
@@ -30,7 +30,7 @@
 def gather_reduce_kernel(
     x, dy, pre, w_in, w_down, dy_all, d_pre, hidden, dx, x_part, x_late0, x_late1, down,
     held, precv, psend, crecv, cs,
-    ws, ios, hos, prs, ls, lr, ps, pr, xls, xlr, xps, xpr, pss, psr, css, csr, fas, fbs, fos, credit,
+    ws, ios, hos, prs, ls, lr, ps, pr, xls, xlr, xps, xpr, pss, psr, css, csr, fas, fbs, fos, dxs, credit,
 ):
     R, D = dy.shape
     F = pre.shape[1]
@@ -59,27 +59,29 @@
         )
 
     def line(way, hop, s, q, own=False):
-        here = dy_all.at[rows(s, c), chunk(q)]
-        src = dy.at[:, chunk(q)] if own else here
-        return remote(src, here, ls.at[way, hop, q], lr.at[s, q], t + 2 - 4 * way)
+        cols = pl.ds(0, D) if q is None else chunk(q)
+        here = dy_all.at[rows(s, c), cols]
+        src = dy.at[:, cols] if own else here
+        return remote(src, here, ls.at[way, hop], lr.at[s, 0 if q is None else q], t + 2 - 4 * way)
 
     def across(s, q, own=False):
-        here = dy_all.at[rows(s, c), chunk(q)]
-        src = dy.at[:, chunk(q)] if own else here
-        return remote(src, here, ps.at[s, q], pr.at[s, q], partner)
+        cols = pl.ds(0, D) if q is None else chunk(q)
+        here = dy_all.at[rows(s, c), cols]
+        src = dy.at[:, cols] if own else here
+        return remote(src, here, ps.at[s], pr.at[s], partner)
 
     def xcols(q):
-        return pl.ds(pl.multiple_of(q * XC, XC), XC)
+        return pl.ds(0, XC * XG) if q is None else pl.ds(pl.multiple_of(q * XC, XC), XC)
 
     def x_line(way, hop, s, q, own=False):
         here = x_part.at[rows(s, c), xcols(q)]
         src = x.at[:, xcols(q)] if own else here
-        return remote(src, here, xls.at[way, hop, q], xlr.at[s, q], t + 2 - 4 * way)
+        return remote(src, here, xls.at[way, hop], xlr.at[s, 0 if q is None else q], t + 2 - 4 * way)
 
     def x_across(s, q, own=False):
         here = x_part.at[rows(s, c), xcols(q)]
         src = x.at[:, xcols(q)] if own else here
-        return remote(src, here, xps.at[s, q], xpr.at[s, q], partner)
+        return remote(src, here, xps.at[s], xpr.at[s], partner)
 
     def send_own(along, over, q):
         over(z, q, own=True).start()
@@ -113,19 +115,19 @@
 
             over(z + hop, q).start()
 
-    def drain(along, over, q):
+    def drain(along, over):
         for hop in range(3):
 
             @pl.when(jnp.logical_and(z >= hop, z < 3))
             def _():
-                along(0, hop, z, q).wait_send()
+                along(0, hop, z, None).wait_send()
 
             @pl.when(jnp.logical_and(z + hop <= 3, z > 0))
             def _():
-                along(1, hop, z, q).wait_send()
+                along(1, hop, z, None).wait_send()
 
         for s in range(4):
-            over(s, q).wait_send()
+            over(s, None).wait_send()
 
     def pair(k, g):
         return remote(
@@ -176,10 +178,22 @@
 
             strips(step)
 
-    def arrive(way, a, g, forward, sent_before):
+    def finished(g):
+        return pltpu.make_async_copy(psend.at[:, slab(g)], dx.at[:, slab(g)], dxs.at[g])
+
+    def arrive(way, a, g, forward, sent_before, last=False):
         d = a + way * (3 - 2 * a)
         chain(way, a, g).wait_recv()
         old = (a - 1) % 2
+        if last:
+
+            def step(r):
+                total = held[d, r, slab(g)] + crecv[way, old, r, slab(g)].astype(F32)
+                psend[r, slab(g)] = total.astype(BF16)
+
+            strips(step)
+            finished(g).start()
+            return
 
         @pl.when(forward)
         def _():
@@ -241,10 +255,10 @@
                 arrive(z - 1, k - 1, v + 3, k == 3, False)
 
     def tail_hooks(f):
-        def sums(j, way, a, forward, sent_before):
+        def sums(j, way, a, forward, sent_before, last=False):
             @pl.loop(0, 2)
             def _(i):
-                arrive(way, a, 2 * j + i, forward, sent_before)
+                arrive(way, a, 2 * j + i, forward, sent_before, last)
 
         @pl.when(middle)
         def _():
@@ -264,7 +278,17 @@
 
                     @pl.when(g < GC)
                     def _():
-                        arrive(2 - z, 2, g, False, False)
+                        arrive(2 - z, 2, g, False, False, last=True)
+
+        @pl.when(f == 1)
+        def _():
+            drain(line, across)
+
+        @pl.when(f == 13)
+        def _():
+            drain(x_line, x_across)
+            for s in range(4):
+                x_across(s, None).wait_recv()
 
         @pl.when(ends)
         def _():
@@ -289,7 +313,7 @@
 
             @pl.when(jnp.logical_and(jnp.logical_and(f >= 8, f <= 15), f % 3 != 1))
             def _():
-                sums(2 * ((f - 8) // 3) + (f - 8) % 3, (3 - z) // 3, 3, False, False)
+                sums(2 * ((f - 8) // 3) + (f - 8) % 3, (3 - z) // 3, 3, False, False, last=True)
 
     barrier = pltpu.get_barrier_semaphore()
     pl.semaphore_signal(barrier, inc=1, device_id={"tp": partner}, device_id_type=pl.DeviceIdType.MESH)
@@ -405,9 +429,7 @@
             def _():
                 pltpu.make_async_copy(dy_all.at[rows(s, c), :], dyv.at[pl.ds(0, R), :], ios.at[0]).start()
 
-            @pl.loop(0, G)
-            def _(q):
-                across(s, q).wait_recv()
+            across(s, None).wait_recv()
 
             other = pltpu.make_async_copy(dy_all.at[rows(s, 1 - c), :], dyv.at[pl.ds(R, R), :], ios.at[1])
             other.start()
@@ -525,6 +547,10 @@
         pltpu.VMEM((2 * R, T), F32),
     )
 
+    @pl.loop(0, G)
+    def _(g):
+        pair(jnp.int32(3), g).wait_send()
+
     TI, TJ = F // BI, D // BJ
 
     def fill(fa, fb, fo):
@@ -587,19 +613,7 @@
     def _():
         @pl.loop(GC - 2, GC)
         def _(g):
-            arrive((3 - z) // 3, 3, g, False, False)
-
-    @pl.loop(0, G)
-    def _(g):
-        pair(jnp.int32(3), g).wait_send()
-
-        def step(r):
-            psend[r, chunk(g)] = held[z, r, chunk(g)].astype(BF16)
-
-        strips(step)
-
-    out = pltpu.make_async_copy(psend, dx, ios.at[0])
-    out.start()
+            arrive((3 - z) // 3, 3, g, False, False, last=True)
 
     @pl.loop(0, GC)
     def _(q):
@@ -612,17 +626,7 @@
         def _():
             chain(z // 3, 3, q).wait_send()
 
-    @pl.loop(0, G)
-    def _(q):
-        drain(line, across, q)
-
-    @pl.loop(0, XG)
-    def _(q):
-        drain(x_line, x_across, q)
-        for s in range(4):
-            x_across(s, q).wait_recv()
-
-    out.wait()
+        finished(q).wait()
 
 
 def gather_reduce(x, dy, pre, w_in, w_down):
@@ -656,14 +660,14 @@
             dma((4,)),
             dma((2, 2)),
             dma((2, 2)),
-            dma((2, 3, G)),
+            dma((2, 3)),
             dma((4, G)),
-            dma((4, G)),
-            dma((4, G)),
-            dma((2, 3, XG)),
+            dma((4,)),
+            dma((4,)),
+            dma((2, 3)),
             dma((4, XG)),
-            dma((4, XG)),
-            dma((4, XG)),
+            dma((4,)),
+            dma((4,)),
             dma((G,)),
             dma((G,)),
             dma((2, GC)),
@@ -671,6 +675,7 @@
             dma((2,)),
             dma((2,)),
             dma((2,)),
+            dma((GC,)),
             pltpu.SemaphoreType.REGULAR,
         ],
         compiler_params=pltpu.CompilerParams(
@@ -730,11 +735,39 @@
 
     @pl.when(n == steps - 1)
     def _():
-        if steps > 1:
-            out(n - 1).wait()
+        out(n - 1).wait()
         out(n).wait()
         if small:
             tiny_out.wait()
+
+
+def plain_grad_kernel(a, b, into, o):
+    o[...] = lax.dot_general(a[...], b[...], TN, preferred_element_type=F32).astype(BF16)
+
+
+def plain_grad(a, b, into, start, bm, bn):
+    rows, A = a.shape
+    B = b.shape[1]
+    off = start // bm
+    return pl.pallas_call(
+        plain_grad_kernel,
+        name="plain_grad",
+        grid=(B // bn, A // bm),
+        out_shape=jax.ShapeDtypeStruct(into.shape, BF16),
+        in_specs=[
+            pl.BlockSpec((rows, bm), lambda j, i: (0, i)),
+            pl.BlockSpec((rows, bn), lambda j, i: (0, j)),
+            pl.BlockSpec(memory_space=pl.ANY),
+        ],
+        out_specs=pl.BlockSpec((bm, bn), lambda j, i: (i + off, j)),
+        input_output_aliases={2: 0},
+        compiler_params=pltpu.CompilerParams(
+            dimension_semantics=("arbitrary", "arbitrary"), vmem_limit_bytes=VMEM
+        ),
+        cost_estimate=pl.CostEstimate(
+            flops=2 * rows * A * B, bytes_accessed=2 * (rows * (A + B) + A * B), transcendentals=0
+        ),
+    )(a, b, into)
 
 
 def weight_grad(a, b, total, into, start, bm, bn, source, target, first, last, small=None):
@@ -801,11 +834,9 @@
             x_part, d_pre, D, None, 0, 512, 3584, down, None, 0, 2304, small=dx
         )
         dw_in, dw_down = weight_grad(
-            late[0], d_pre, D, dw_in, XW, 512, 3584, down, dw_down, 2304, 3328
+            late[0], d_pre, D, dw_in, XW, 512, 3584, down, dw_down, 2304, F
         )
-        dw_in, dw_down = weight_grad(
-            late[1], d_pre, D, dw_in, XW + XL, 512, 896, down, dw_down, 3328, F
-        )
+        dw_in = plain_grad(late[1], d_pre, dw_in, XW + XL, 512, 1792)
         return dx, dw_in, dw_down
 
     rows = P(("dp", "tp"), None)

time: 413 us -> 408 us (0.988)
    pallas_call x3 -> x2, Pallas kernels: 94.7 us -> 83.9 us  [weight_grad(): pl.pallas_call(functools.partial(weight_grad_kernel, first=first, size=si...]
    pallas_call x0 -> x1, Pallas kernels: none -> 9.14 us  [plain_grad(): pl.pallas_call(plain_grad_kernel, name='plain_grad', grid=(B // bn, A //...]
  transfers between devices with their start and end apart: 2 -> 2, of which waited for: 1 -> 1; matrix products, arithmetic and copies ran while one was open for 0% -> 0% of each run, Pallas kernels for 20% -> 21%
where the time goes in v4:
time: 408 us
  Pallas kernels  393 us (96%)
  between operations  14.1 us (3%)
    pallas_call x1, Pallas kernels, gather_reduce(): pl.pallas_call(gather_reduce_kernel, name='gather_reduce', out_shape=(jax...  300 us
    pallas_call x2, Pallas kernels, weight_grad(): pl.pallas_call(functools.partial(weight_grad_kernel, first=first, size=si...  83.9 us
    pallas_call x1, Pallas kernels, plain_grad(): pl.pallas_call(plain_grad_kernel, name='plain_grad', grid=(B // bn, A //...  9.14 us
  transfers between devices with their start and end apart: 2, of which 1 were waited for; matrix products, arithmetic and copies ran while one was open for 0% of the time, Pallas kernels for 21%

profile of v4, /device:TPU:0, one launch (start us, length us, event | category | flops | bytes accessed | tf_op | source)
XLA Modules:
  0.0 408.1 jit_solution(12697575577269402144)
XLA Ops:
  7.2 0.0 all-gather.5.cloned.1.call-start
  7.2 299.6 %gather_reduce.1 = (bf16[1280,7168]{1,0:T(8,128)(2,1)}, bf16[1280,3584]{1,0:T(8,128)(2,1)}, bf16[1280,3584]{1,0:T(8,128)(2,1)}, bf16[160,7168]{1,0:T(8,128)(2,1)...) custom-call(bf16[160,7168]{1,0:T(8,128)(2,1)} %x.1, ...), custom_call_target="tpu_custom_call" | custom-call | flops 131533373440 | bytes 411041792 | tf_op jit(solution)/shard_map/gather_reduce/pallas_call | solution.py:638
  306.8 0.0 all-gather.5.cloned.1.call-update
  306.8 0.2 all-gather.3.cloned.1.call-start
  307.1 0.5 all-gather.3.cloned.1.call-update
  307.6 54.9 %weight_grad.2 = (bf16[7168,3584]{1,0:T(8,128)(2,1)}, bf16[3584,7168]{1,0:T(8,128)(2,1)}, bf16[160,7168]{1,0:T(8,128)(2,1)}) custom-call(bf16[1280,4608]{1,0:T(8,128)(2,1)} %get-tuple-element.14.a, bf16[1280,3584]{1,0:T(8,128)(2,1)} %get-tuple-element.15.b, bf16[3584,7168]{1,0:T(8,128)(2,1)} %get-tuple-element.16.source, ...), custom_call_target="tpu_custom_call" | custom-call | flops 42278584320 | bytes 54001664 | tf_op jit(solution)/shard_map/weight_grad/pallas_call | solution.py:799
  362.5 0.6 all-gather.5.cloned.1.call-done.a
  363.1 29.0 %weight_grad.3 = (bf16[7168,3584]{1,0:T(8,128)(2,1)}, bf16[3584,7168]{1,0:T(8,128)(2,1)}) custom-call(bf16[1280,2048]{1,0:T(8,128)(2,1)} %all-gather.5.cloned.1.call-done.a, bf16[1280,3584]{1,0:T(8,128)(2,1)} %get-tuple-element.15.b, bf16[3584,7168]{1,0:T(8,128)(2,1)} %get-tuple-element.16.source, ...), custom_call_target="tpu_custom_call", output_to_operand_aliasing={{0}: (3, {}), {1}: (4, {})} | custom-call | flops 18790481920 | bytes 29097984 | tf_op jit(solution)/shard_map/weight_grad/pallas_call | solution.py:799
  392.1 0.0 all-gather.3.cloned.1.call-done.a
  392.1 9.1 %plain_grad.1 = bf16[7168,3584]{1,0:T(8,128)(2,1)} custom-call(bf16[1280,512]{1,0:T(8,128)(2,1)} %all-gather.3.cloned.1.call-done.a, bf16[1280,3584]{1,0:T(8,128)(2,1)} %get-tuple-element.15.b, bf16[7168,3584]{1,0:T(8,128)(2,1)} %get-tuple-element.23.into), custom_call_target="tpu_custom_call", output_to_operand_aliasing={{}: (2, {})} | custom-call | flops 4697620480 | bytes 14155776 | tf_op jit(solution)/shard_map/plain_grad/pallas_call | solution.py:752
Async XLA Ops:
  7.2 355.9 %all-gather.5.cloned.1.call-start = ((), (), s32[]{:S(2)}) async-start(), calls=%async_computation.1 | async-start | bytes 5898240 | tf_op jit(solution)/shard_map/all_gather | solution.py:831
  306.8 85.3 %all-gather.3.cloned.1.call-start = ((), (), s32[]{:S(2)}) async-start(), calls=%async_computation | async-start | bytes 1474560 | tf_op jit(solution)/shard_map/all_gather | solution.py:831
Sparse Core Ops, SparseCore 0:
  307.0 56.0 all-gather.4
  364.7 22.1 all-gather.2
